TPU v7x, 32 devices: a 4x4x1 block of a 4x4x8 slice. The times are simulated.
32 devices in a mesh: inst: 1 (over z), qy: 4 (over y), qx: 8 (over x, core).
Axes of the slice: x: 4, y: 4, z: 1, core: 2. Of those that a mesh axis runs over, the one named last changes fastest.
The devices are a block of a 4x4x8 slice.
Arguments:
- cost_diag: float32 [2097152], P(('inst', 'qy', 'qx'))
- gamma_angles: float32 [8], replicated
- beta_angles: float32 [8], replicated
Outputs:
- output 1: float32 [1], P('inst')
- output 2: float32 [16], P('inst')
- output 3: float32 [2, 2097152], P(None, ('inst', 'qy', 'qx'))
All inputs are finite; a program needn't handle non-finite values.
Results may differ from a plain program's by a relative error of at most 0.001.
Values sent between devices are 32-bit elements.
A program may use at most 768 MiB of HBM per device.

v0:
```python
import math
import jax
import jax.numpy as jnp
from jax import lax
from jax.sharding import PartitionSpec as P


def turn_vec(state_vec):
    return jnp.stack([state_vec[1], -state_vec[0]])


def phase_turn(state_vec, cost_rows, angle, sign_flip):
    phase_angle = angle * cost_rows
    cos_phase = jnp.cos(phase_angle)
    sin_phase = sign_flip * jnp.sin(phase_angle)
    return jnp.stack([cos_phase * state_vec[0] + sin_phase * state_vec[1], cos_phase * state_vec[1] - sin_phase * state_vec[0]])


def pair_swap(state_vec, qubit_num):
    if qubit_num < 7:
        pair_dist = 2 ** qubit_num
        lane_ids = lax.broadcasted_iota(jnp.int32, (1, 128), 1)
        upper_half = jnp.bitwise_and(lane_ids, pair_dist) > 0
        return jnp.where(upper_half, jnp.roll(state_vec, pair_dist, axis=-1), jnp.roll(state_vec, -pair_dist, axis=-1))
    pair_dist = 2 ** (qubit_num - 7)
    num_rows = state_vec.shape[-2]
    if pair_dist < 8:
        row_ids = lax.broadcasted_iota(jnp.int32, (num_rows, 1), 0)
        upper_half = jnp.bitwise_and(row_ids, pair_dist) > 0
        return jnp.where(upper_half, jnp.roll(state_vec, pair_dist, axis=-2), jnp.roll(state_vec, -pair_dist, axis=-2))
    split_view = state_vec.reshape(state_vec.shape[:-2] + (num_rows // (2 * pair_dist), 2, pair_dist, 128))
    return jnp.flip(split_view, axis=-3).reshape(state_vec.shape)


def mix_qubit(state_vec, qubit_num, cos_half, sin_half):
    return cos_half * state_vec + sin_half * turn_vec(pair_swap(state_vec, qubit_num))


def unmix_qubit(both_vecs, qubit_num, cos_half, sin_half):
    partner = pair_swap(both_vecs, qubit_num)
    beta_term = jnp.sum(both_vecs[0, 1] * partner[1, 0] - both_vecs[1, 1] * partner[0, 0], axis=(-2, -1))
    return cos_half * both_vecs - sin_half * turn_vec(partner), beta_term


def solution(mesh):
    qy_size = mesh.shape["qy"]
    qx_size = mesh.shape["qx"]
    global_steps = [("qx", qx_size, 2 ** bit_pos) for bit_pos in range(int(math.log2(qx_size)))] + [("qy", qy_size, 2 ** bit_pos) for bit_pos in range(int(math.log2(qy_size)))]

    def partner_block(payload, axis_name, axis_size, mask_bit):
        return lax.ppermute(payload, axis_name, [(position, position ^ mask_bit) for position in range(axis_size)])

    def local_run(cost_local, gamma_angles, beta_angles):
        chunk_len = cost_local.shape[0]
        local_qubits = int(math.log2(chunk_len))
        num_layers = gamma_angles.shape[0]
        total_len = chunk_len * qy_size * qx_size
        cost_rows = cost_local.reshape(chunk_len // 128, 128)
        start_re = jnp.full(cost_rows.shape, total_len ** -0.5, jnp.float32)
        state_vec = jnp.stack([start_re, jnp.zeros_like(start_re)])
        for layer_num in range(num_layers):
            state_vec = phase_turn(state_vec, cost_rows, gamma_angles[layer_num], 1.0)
            cos_half = jnp.cos(0.5 * beta_angles[layer_num])
            sin_half = jnp.sin(0.5 * beta_angles[layer_num])
            for qubit_num in range(local_qubits):
                state_vec = mix_qubit(state_vec, qubit_num, cos_half, sin_half)
            for axis_name, axis_size, mask_bit in global_steps:
                partner = partner_block(state_vec, axis_name, axis_size, mask_bit)
                state_vec = cos_half * state_vec + sin_half * turn_vec(partner)
        energy_part = jnp.sum(cost_rows * (state_vec[0] ** 2 + state_vec[1] ** 2))
        both_vecs = jnp.stack([state_vec, cost_rows * state_vec], axis=1)
        gamma_grads = []
        beta_grads = []
        for layer_num in reversed(range(num_layers)):
            cos_half = jnp.cos(0.5 * beta_angles[layer_num])
            sin_half = jnp.sin(0.5 * beta_angles[layer_num])
            beta_sum = jnp.zeros((), jnp.float32)
            for qubit_num in range(local_qubits):
                both_vecs, beta_term = unmix_qubit(both_vecs, qubit_num, cos_half, sin_half)
                beta_sum = beta_sum + beta_term
            for axis_name, axis_size, mask_bit in global_steps:
                partner = partner_block(both_vecs, axis_name, axis_size, mask_bit)
                beta_sum = beta_sum + jnp.sum(both_vecs[0, 1] * partner[1, 0] - both_vecs[1, 1] * partner[0, 0])
                both_vecs = cos_half * both_vecs - sin_half * turn_vec(partner)
            gamma_sum = 2.0 * jnp.sum(cost_rows * (both_vecs[0, 1] * both_vecs[1, 0] - both_vecs[1, 1] * both_vecs[0, 0]))
            both_vecs = phase_turn(both_vecs, cost_rows, gamma_angles[layer_num], -1.0)
            gamma_grads.append(gamma_sum)
            beta_grads.append(beta_sum)
        partials = jnp.concatenate([energy_part.reshape(1), jnp.stack(gamma_grads[::-1]), jnp.stack(beta_grads[::-1])])
        totals = lax.psum(partials, ("qy", "qx"))
        return totals[:1], totals[1:], (state_vec * total_len ** 0.5).reshape(2, chunk_len)

    state_spec = P(("inst", "qy", "qx"))
    return jax.shard_map(local_run, mesh=mesh, in_specs=(state_spec, P(), P()), out_specs=(P("inst"), P("inst"), P(None, ("inst", "qy", "qx"))), check_vma=False)
```

profile of v0, /device:TPU:97, one launch (start us, length us, event | category | flops | bytes accessed | tf_op | source)
XLA Modules:
  0.0 3006.8 jit_solution(8113491603031172517)
XLA Ops:
  63.1 12.4 collective-permute-done.1
  81.2 11.3 collective-permute-done.2
  97.3 9.8 collective-permute-done.3
  201.2 12.0 collective-permute-done.6
  219.3 10.9 collective-permute-done.7
  234.4 10.4 collective-permute-done.8
  338.1 12.0 collective-permute-done.11
  356.2 10.9 collective-permute-done.12
  371.3 10.4 collective-permute-done.13
  474.7 12.0 collective-permute-done.16
  492.9 10.9 collective-permute-done.17
  507.9 10.4 collective-permute-done.18
  611.5 12.0 collective-permute-done.21
  629.7 10.9 collective-permute-done.22
  644.7 10.4 collective-permute-done.23
  748.0 12.0 collective-permute-done.26
  766.1 10.9 collective-permute-done.27
  781.2 10.4 collective-permute-done.28
  884.9 12.0 collective-permute-done.31
  903.1 10.9 collective-permute-done.32
  918.1 10.4 collective-permute-done.33
  1017.3 12.0 collective-permute-done.36
  1033.4 10.9 collective-permute-done.37
  1048.1 10.4 collective-permute-done.38
  1205.2 23.2 collective-permute-done.41
  1232.5 22.2 collective-permute-done.42
  1256.8 21.6 collective-permute-done.43
  1283.0 12.0 multiply_cosine_fusion.6
  1407.4 23.2 collective-permute-done.46
  1434.8 22.2 collective-permute-done.47
  1459.2 21.6 collective-permute-done.48
  1485.3 20.1 collective-permute-done.49
  1610.0 23.2 collective-permute-done.51
  1637.3 22.2 collective-permute-done.52
  1661.7 21.6 collective-permute-done.53
  1687.8 20.1 collective-permute-done.54
  1812.3 23.2 collective-permute-done.56
  1839.6 22.2 collective-permute-done.57
  1864.0 21.6 collective-permute-done.58
  1890.1 20.1 collective-permute-done.59
  2019.5 18.7 collective-permute-done.61
  2052.1 12.7 collective-permute-done.62
  2122.4 12.2 collective-permute-done.64
  2551.5 13.4 collective-permute-done.71
  2623.3 11.5 collective-permute-done.73
  2878.0 13.2 collective-permute-done.78
  2946.0 15.5 fusion.2972
  2961.5 44.3 %psum.7 = f32[17]{0:T(128)S(1)} all-reduce(f32[17]{0:T(128)S(1)} %concatenate.5620), channel_id=1, replica_groups=mesh['inst'=1,'qy'=4,'qx'=8] {'qy','qx'}, use_global_device_ids=true, to_apply=%region_177.178 | all-reduce | flops 17 | bytes 136 | tf_op jit(solution)/shard_map/psum | solution.py:90
  (3882 shorter events, 2123.6 us)
Async XLA Ops:
  62.2 13.2 collective-permute-start.1
  78.7 13.9 collective-permute-start.2
  199.9 13.2 collective-permute-start.6
  216.4 13.9 collective-permute-start.7
  336.8 13.2 collective-permute-start.11
  353.3 13.9 collective-permute-start.12
  489.9 13.9 collective-permute-start.17
  626.7 13.9 collective-permute-start.22
  746.7 13.2 collective-permute-start.26
  763.2 13.9 collective-permute-start.27
  883.7 13.2 collective-permute-start.31
  900.1 13.9 collective-permute-start.32
  1030.5 13.9 collective-permute-start.37
  1203.9 24.4 collective-permute-start.41
  1229.6 25.1 collective-permute-start.42
  1256.0 22.5 collective-permute-start.43
  1279.9 23.1 collective-permute-start.44
  1406.1 24.4 collective-permute-start.46
  1431.9 25.1 collective-permute-start.47
  1458.3 22.5 collective-permute-start.48
  1482.2 23.1 collective-permute-start.49
  1608.7 24.4 collective-permute-start.51
  1634.4 25.1 collective-permute-start.52
  1660.8 22.5 collective-permute-start.53
  1684.7 23.1 collective-permute-start.54
  1811.0 24.4 collective-permute-start.56
  1836.7 25.1 collective-permute-start.57
  1863.1 22.5 collective-permute-start.58
  1887.0 23.1 collective-permute-start.59
  2013.7 24.4 collective-permute-start.61
  2039.7 25.1 collective-permute-start.62
  2067.0 40.6 %collective-permute-start.63 = (f32[2,2,512,128]{3,2,1,0:T(8,128)}, f32[2,2,512,128]{3,2,1,0:T(8,128)}, u32[]{:S(2)}, u32[]{:S(2)}) collective-permute-start(f32[2,2,512,128]{3,2,1,0:T(8,128)} %fusion.835), channel_id=1, source_target_pairs={{0,8},{8,0},{16,24},{24,16},{1,9},{9,1},{17,25},{25,17},{2,10},{10... | collective-permute-start | bytes 3145736 | tf_op jit(solution)/shard_map/ppermute | solution.py:51
  2110.0 24.6 collective-permute-start.64
  2230.4 39.4 %collective-permute-start.65 = (f32[2,2,512,128]{3,2,1,0:T(8,128)}, f32[2,2,512,128]{3,2,1,0:T(8,128)}, u32[]{:S(2)}, u32[]{:S(2)}) collective-permute-start(f32[2,2,512,128]{3,2,1,0:T(8,128)} %get-tuple-element.28), channel_id=1, source_target_pairs={{0,1},{1,0},{2,3},{3,2},{4,5},{5,4},{6,7},{7,6},{8,9},{9,8},{10,11... | collective-permute-start | bytes 3145736 | tf_op jit(solution)/shard_map/ppermute | solution.py:51
  2273.8 24.5 collective-permute-start.66
  2302.4 42.6 %collective-permute-start.67 = (f32[2,2,512,128]{3,2,1,0:T(8,128)}, f32[2,2,512,128]{3,2,1,0:T(8,128)}, u32[]{:S(2)}, u32[]{:S(2)}) collective-permute-start(f32[2,2,512,128]{3,2,1,0:T(8,128)} %fusion.992), channel_id=1, source_target_pairs={{0,4},{1,5},{2,6},{3,7},{4,0},{5,1},{6,2},{7,3},{8,12},{9,13},{10,... | collective-permute-start | bytes 3145736 | tf_op jit(solution)/shard_map/ppermute | solution.py:51
  2349.3 23.4 collective-permute-start.68
  2377.1 26.3 collective-permute-start.69
  2504.0 33.3 %collective-permute-start.70 = (f32[2,2,512,128]{3,2,1,0:T(8,128)}, f32[2,2,512,128]{3,2,1,0:T(8,128)}, u32[]{:S(2)}, u32[]{:S(2)}) collective-permute-start(f32[2,2,512,128]{3,2,1,0:T(8,128)} %get-tuple-element.21), channel_id=1, source_target_pairs={{0,1},{1,0},{2,3},{3,2},{4,5},{5,4},{6,7},{7,6},{8,9},{9,8},{10,11... | collective-permute-start | bytes 3145736 | tf_op jit(solution)/shard_map/ppermute | solution.py:51
  2540.6 24.4 collective-permute-start.71
  2568.5 39.3 %collective-permute-start.72 = (f32[2,2,512,128]{3,2,1,0:T(8,128)}, f32[2,2,512,128]{3,2,1,0:T(8,128)}, u32[]{:S(2)}, u32[]{:S(2)}) collective-permute-start(f32[2,2,512,128]{3,2,1,0:T(8,128)} %fusion.1150), channel_id=1, source_target_pairs={{0,4},{1,5},{2,6},{3,7},{4,0},{5,1},{6,2},{7,3},{8,12},{9,13},{10,... | collective-permute-start | bytes 3145736 | tf_op jit(solution)/shard_map/ppermute | solution.py:51
  2611.3 23.5 collective-permute-start.73
  2638.6 41.0 %collective-permute-start.74 = (f32[2,2,512,128]{3,2,1,0:T(8,128)}, f32[2,2,512,128]{3,2,1,0:T(8,128)}, u32[]{:S(2)}, u32[]{:S(2)}) collective-permute-start(f32[2,2,512,128]{3,2,1,0:T(8,128)} %fusion.1152), channel_id=1, source_target_pairs={{0,16},{8,24},{16,0},{24,8},{1,17},{9,25},{17,1},{25,9},{2,18},{10... | collective-permute-start | bytes 3145736 | tf_op jit(solution)/shard_map/ppermute | solution.py:51
  2779.3 20.0 collective-permute-start.75
  2803.4 24.8 collective-permute-start.76
  2832.3 31.6 %collective-permute-start.77 = (f32[2,2,512,128]{3,2,1,0:T(8,128)}, f32[2,2,512,128]{3,2,1,0:T(8,128)}, u32[]{:S(2)}, u32[]{:S(2)}) collective-permute-start(f32[2,2,512,128]{3,2,1,0:T(8,128)} %fusion.1308), channel_id=1, source_target_pairs={{0,4},{1,5},{2,6},{3,7},{4,0},{5,1},{6,2},{7,3},{8,12},{9,13},{10,... | collective-permute-start | bytes 3145736 | tf_op jit(solution)/shard_map/ppermute | solution.py:51
  2867.5 23.8 collective-permute-start.78
  2894.8 40.3 %collective-permute-start.79 = (f32[2,2,512,128]{3,2,1,0:T(8,128)}, f32[2,2,512,128]{3,2,1,0:T(8,128)}, u32[]{:S(2)}, u32[]{:S(2)}) collective-permute-start(f32[2,2,512,128]{3,2,1,0:T(8,128)} %fusion.1310), channel_id=1, source_target_pairs={{0,16},{8,24},{16,0},{24,8},{1,17},{9,25},{17,1},{25,9},{2,18},{10... | collective-permute-start | bytes 3145736 | tf_op jit(solution)/shard_map/ppermute | solution.py:51
  (1142 other events, 10475.5 us)
where the time goes:
time: 3030 us; the launch traced here: 3010 us
  other arithmetic  1230 us (41%)
  waiting for transfers between devices  791 us (26%)
  local copies, waits for them, and re-layouts  621 us (20%)
  starting transfers between devices  185 us (6%)
  between operations  135 us (4%)
  blocking collectives  44.3 us (1%)
    ppermute x80, waiting for transfers between devices, partner_block(): lax.ppermute(payload, axis_name, [(position, position ^ mask_bit) for pos...  791 us
    sub x128, other arithmetic, unmix_qubit(): return (cos_half * both_vecs - sin_half * turn_vec(partner), beta_term)  294 us
    slice x192, local copies, waits for them, and re-layouts, turn_vec(): return jnp.stack([state_vec[1], -state_vec[0]])  266 us
    unnamed x2220, local copies, waits for them, and re-layouts  213 us
    add x128, other arithmetic, mix_qubit(): cos_half * state_vec + sin_half * turn_vec(pair_swap(state_vec, qubit_num))  202 us
    ppermute x80, starting transfers between devices, partner_block(): lax.ppermute(payload, axis_name, [(position, position ^ mask_bit) for pos...  185 us
    reduce_sum x104, other arithmetic, unmix_qubit(): jnp.sum(both_vecs[0, 1] * partner[1, 0] - both_vecs[1, 1] * partner[0, 0]...  165 us
    add x39, other arithmetic, local_run(): state_vec = cos_half * state_vec + sin_half * turn_vec(partner)  120 us
  transfers between devices with their start and end apart: 80, of which 70 were waited for; matrix products, arithmetic and copies ran while one was open for 11% of the time, Pallas kernels for 0%

commit v1 on v0

v1 whole, which is shorter than its diff:
```python
import functools
import math

import jax
import jax.numpy as jnp
from jax import lax
from jax.experimental import pallas as pl
from jax.experimental.pallas import tpu as pltpu
from jax.sharding import PartitionSpec as P

LANES = 128
MESH_ID = pl.DeviceIdType.MESH


def mix_pair(blocks, tan_half, stride):
    out = list(blocks)
    for low in range(len(blocks)):
        if low & stride:
            continue
        high = low | stride
        (re0, im0), (re1, im1) = blocks[low], blocks[high]
        out[low] = (re0 + tan_half * im1, im0 - tan_half * re1)
        out[high] = (re1 + tan_half * im0, im1 - tan_half * re0)
    return out


def mix_all(blocks, tan_half):
    stride = 1
    while stride < len(blocks):
        blocks = mix_pair(blocks, tan_half, stride)
        stride *= 2
    return blocks


def partner_sums(blocks):
    out = []
    for place in range(len(blocks)):
        stride, re, im = 1, None, None
        while stride < len(blocks):
            pre, pim = blocks[place ^ stride]
            re, im = (pre, pim) if re is None else (re + pre, im + pim)
            stride *= 2
        out.append((re, im))
    return out


def inner_partners(tiles, per_block, apply):
    lane = lax.broadcasted_iota(jnp.int32, (1, 8, LANES), 2)
    sub = lax.broadcasted_iota(jnp.int32, (1, 8, LANES), 1)

    def rolled(x, ids, dist, axis, size):
        if 2 * dist == size:
            return pltpu.roll(x, dist, axis)
        upper = (ids // dist) % 2 > 0
        return jnp.where(upper, pltpu.roll(x, dist, axis), pltpu.roll(x, size - dist, axis))

    for bit in range(7):
        tiles = apply(tiles, lambda x, d=2 ** bit: rolled(x, lane, d, 2, LANES))
    for bit in range(3):
        tiles = apply(tiles, lambda x, d=2 ** bit: rolled(x, sub, d, 1, 8))
    stride = 1
    while stride < per_block:
        def swapped(x, d=stride):
            return jnp.concatenate([x[(i ^ d):(i ^ d) + 1] for i in range(x.shape[0])], axis=0)
        tiles = apply(tiles, swapped)
        stride *= 2
    return tiles


def kernel(ny, nx, num_layers, num_qubits, amp, cost, gamma, beta, final, totals,
           cost_b, tabs, post, pre, recv, send, work, lam, lam_pre, qbuf, angle, acc, part, gath,
           send_sem, recv_sem, cost_send, cost_recv, sum_send, sum_recv):
    nb = ny * nx
    chips = nx // 2
    rows = cost.shape[1]
    tiles = rows // 8
    my_y = lax.axis_index("qy")
    my_x = lax.axis_index("qx")
    my_chip, my_core = my_x // 2, my_x % 2
    me = my_y * nx + my_x

    def peer(dy, dx, dc):
        y = (my_y + dy) % ny
        x = ((my_chip + dx) % chips) * 2 + (my_core + dc) % 2
        return y, x, y * nx + x

    dy_order = sorted(range(ny), key=lambda d: -min(d, ny - d))
    dx_order = sorted(range(chips), key=lambda d: -min(d, chips - d))
    offsets = [(dy, dx, dc) for dy in dy_order for dx in dx_order for dc in (1, 0)]

    barrier = pltpu.get_barrier_semaphore()
    for dy, dx, dc in offsets:
        if dy or dx or dc:
            y, x, _ = peer(dy, dx, dc)
            pl.semaphore_signal(barrier, inc=1, device_id={"qy": y, "qx": x}, device_id_type=MESH_ID)

    for layer in range(num_layers):
        half = jnp.full((8, LANES), 0.5 * beta[layer], jnp.float32)
        cos_half, sin_half = jnp.cos(half), jnp.sin(half)
        scale, power, left = None, cos_half, num_qubits
        while left:
            if left % 2:
                scale = power if scale is None else scale * power
            power, left = power * power, left // 2
        angle[layer, 0] = sin_half / cos_half
        angle[layer, 1] = scale

    def angle_of(layer, kind):
        tile = angle[layer, kind]
        return jnp.concatenate([tile] * tiles, axis=0) if tiles > 1 else tile

    def make_table(layer, source):
        g = gamma[layer]

        def body(j, _):
            theta = g * source[j]
            tabs[layer, 0, j] = jnp.cos(theta)
            tabs[layer, 1, j] = jnp.sin(theta)
            return 0

        lax.fori_loop(0, nb, body, 0)

    def turn(block, layer, j, sign):
        re, im = block
        c, s = tabs[layer, 0, j], sign * tabs[layer, 1, j]
        return c * re + s * im, c * im - s * re

    def low_bits(src, dst, tan_half, y):
        blocks = [(src[y * nx + x, 0], src[y * nx + x, 1]) for x in range(nx)]
        for x, (re, im) in enumerate(mix_all(blocks, tan_half)):
            dst[y * nx + x, 0] = re
            dst[y * nx + x, 1] = im

    def start_send(par, dy, dx, dc):
        y, x, dest = peer(dy, dx, dc)
        if not (dy or dx or dc):
            pltpu.make_async_copy(send.at[par, me], recv.at[par, me], recv_sem.at[par, me]).start()
            return
        pltpu.make_async_remote_copy(
            src_ref=send.at[par, dest], dst_ref=recv.at[par, me],
            send_sem=send_sem.at[par], recv_sem=recv_sem.at[par, me],
            device_id={"qy": y, "qx": x}, device_id_type=MESH_ID).start()

    def wait_sends(par):
        view = send.at[par, pl.ds(0, nb - 1)]
        pltpu.make_async_copy(view, view, send_sem.at[par]).wait()

    def low_bits_and_send(par, tan_half):
        for dy in dy_order:
            y = (my_y + dy) % ny
            low_bits(work, send.at[par], tan_half, y)
            for dx in dx_order:
                for dc in (1, 0):
                    start_send(par, dy, dx, dc)

    groups = (nb + 3) // 4

    def receive(par, tan_half):
        tile = tan_half[:8].reshape(1, 8, LANES)

        def body(i, _):
            slots = []
            for k in range(nb // groups):
                n = i * (nb // groups) + k
                dy = (n // nx + ny // 2) % ny
                dx = ((n % nx) // 2 + chips // 2) % chips
                _, _, slot = peer(dy, dx, n % 2)
                view = recv.at[par, slot]
                pltpu.make_async_copy(view, view, recv_sem.at[par, slot]).wait()
                slots.append(slot)
            re = jnp.concatenate([recv[par, s, 0].reshape(tiles, 8, LANES) for s in slots], axis=0)
            im = jnp.concatenate([recv[par, s, 1].reshape(tiles, 8, LANES) for s in slots], axis=0)
            re, im = inner_partners((re, im), tiles, lambda t, f: (t[0] + tile * f(t[1]), t[1] - tile * f(t[0])))
            for k, s in enumerate(slots):
                recv[par, s, 0] = re[k * tiles:(k + 1) * tiles].reshape(rows, LANES)
                recv[par, s, 1] = im[k * tiles:(k + 1) * tiles].reshape(rows, LANES)
            return 0

        lax.fori_loop(0, groups, body, 0)

    def all_low_bits(par, tan_half):
        def body(y, _):
            low_bits(recv.at[par], work, tan_half, y)
            return 0
        lax.fori_loop(0, ny, body, 0)

    def column(x):
        return [y * nx + x for y in range(ny)]

    def load(ref, places):
        return [(ref[j, 0], ref[j, 1]) for j in places]

    def store(ref, places, blocks):
        for j, (re, im) in zip(places, blocks):
            ref[j, 0] = re
            ref[j, 1] = im

    def for_columns(body):
        lax.fori_loop(0, nx, lambda x, _: (body(column(x)), 0)[1], 0)

    def scaled(blocks, scale):
        return [(scale * re, scale * im) for re, im in blocks]

    make_table(0, cost)
    tan0 = angle_of(0, 0)

    def first(places):
        flat = jnp.full((rows, LANES), amp, jnp.float32)
        blocks = [(flat, jnp.zeros_like(flat)) for _ in places]
        blocks = [turn(b, 0, j, 1.0) for b, j in zip(blocks, places)]
        store(pre.at[0], places, blocks)
        store(work, places, mix_all(blocks, tan0))

    for_columns(first)
    for place in range(acc.shape[0]):
        acc[place] = jnp.zeros((8, LANES), jnp.float32)

    pl.semaphore_wait(barrier, nb - 1)

    for dy, dx, dc in offsets:
        y, x, dest = peer(dy, dx, dc)
        if dy or dx or dc:
            pltpu.make_async_remote_copy(
                src_ref=cost.at[dest], dst_ref=cost_b.at[me], send_sem=cost_send, recv_sem=cost_recv.at[me],
                device_id={"qy": y, "qx": x}, device_id_type=MESH_ID).start()
        else:
            pltpu.make_async_copy(cost.at[me], cost_b.at[me], cost_recv.at[me]).start()
    low_bits_and_send(0, tan0)

    def cost_wait(j, _):
        pltpu.make_async_copy(cost_b.at[j], cost_b.at[j], cost_recv.at[j]).wait()
        return 0

    lax.fori_loop(0, nb, cost_wait, 0)

    def forward(layer, _):
        par = layer % 2

        @pl.when(par == 0)
        def _():
            make_table(layer + 1, cost_b)

        @pl.when(par == 1)
        def _():
            make_table(layer + 1, cost)

        tan_half, scale = angle_of(layer, 0), angle_of(layer, 1)
        tan_next = angle_of(layer + 1, 0)
        receive(par, tan_half)
        all_low_bits(par, tan_half)

        def middle(places):
            blocks = scaled(mix_all(load(work, places), tan_half), scale)
            store(post.at[layer], places, blocks)
            blocks = [turn(b, layer + 1, j, 1.0) for b, j in zip(blocks, places)]
            store(pre.at[layer + 1], places, blocks)
            store(work, places, mix_all(blocks, tan_next))

        for_columns(middle)

        @pl.when(layer > 0)
        def _():
            wait_sends(1 - par)

        low_bits_and_send(1 - par, tan_next)
        return 0

    lax.fori_loop(0, num_layers - 1, forward, 0)

    last = num_layers - 1
    par = last % 2
    tan_half, scale = angle_of(last, 0), angle_of(last, 1)
    receive(par, tan_half)
    all_low_bits(par, tan_half)
    root = jnp.float32(1.0 / amp)

    def turn_point(places):
        blocks = scaled(mix_all(load(work, places), tan_half), scale)
        store(post.at[last], places, blocks)
        turned = []
        energy = acc[0]
        for j, (re, im) in zip(places, blocks):
            c = cost[j]
            final[0, j] = root * re
            final[1, j] = root * im
            turned.append((c * re, c * im))
            energy += (c * (re * re + im * im)).reshape(tiles, 8, LANES).sum(axis=0)
        acc[0] = energy
        store(lam, places, turned)
        store(work, places, mix_all(turned, -tan_half))

    for_columns(turn_point)
    wait_sends(1 - par)
    low_bits_and_send(1 - par, -tan_half)

    def im_dot(left, right):
        return (left[0] * right[1] - left[1] * right[0]).reshape(tiles, 8, LANES).sum(axis=0)

    def block_sums(src):
        def low(y, _):
            places = [y * nx + x for x in range(nx)]
            store(qbuf, places, partner_sums(load(src, places)))
            return 0

        lax.fori_loop(0, ny, low, 0)

        def high(places):
            sums = partner_sums(load(src, places))
            store(qbuf, places, [(a + c, b + d) for (a, b), (c, d) in zip(sums, load(qbuf, places))])

        for_columns(high)

    def inner_sums(src):
        def body(j, _):
            x = (src[j, 0].reshape(tiles, 8, LANES), src[j, 1].reshape(tiles, 8, LANES))
            total = (qbuf[j, 0].reshape(tiles, 8, LANES), qbuf[j, 1].reshape(tiles, 8, LANES))
            parts = []
            inner_partners(x, tiles, lambda t, f: (parts.append((f(t[0]), f(t[1]))), t)[1])
            for re, im in parts:
                total = (total[0] + re, total[1] + im)
            qbuf[j, 0] = total[0].reshape(rows, LANES)
            qbuf[j, 1] = total[1].reshape(rows, LANES)
            return 0

        lax.fori_loop(0, nb, body, 0)

    def dot_with_sums(left):
        def body(j, total):
            return total + im_dot((left[j, 0], left[j, 1]), (qbuf[j, 0], qbuf[j, 1]))
        return lax.fori_loop(0, nb, body, jnp.zeros((8, LANES), jnp.float32))

    def backward(step, _):
        layer = last - step
        par = layer % 2
        back = 1 - par
        block_sums(post.at[layer])
        beta_part = dot_with_sums(lam)
        block_sums(pre.at[layer])
        inner_sums(pre.at[layer])

        tan_half, scale = -angle_of(layer, 0), angle_of(layer, 1)
        receive(back, tan_half)
        all_low_bits(back, tan_half)

        before = lax.max(layer - 1, 0)
        tan_next = -angle_of(before, 0)

        def middle(places):
            blocks = scaled(mix_all(load(work, places), tan_half), scale)
            store(lam_pre, places, blocks)
            blocks = [turn(b, layer, j, -1.0) for b, j in zip(blocks, places)]
            store(lam, places, blocks)
            store(work, places, mix_all(blocks, tan_next))

        for_columns(middle)
        wait_sends(par)

        @pl.when(layer > 0)
        def _():
            low_bits_and_send(par, tan_next)

        beta_part += dot_with_sums(lam_pre)

        def gamma_body(j, total):
            prod = lam_pre[j, 0] * pre[layer, j, 1] - lam_pre[j, 1] * pre[layer, j, 0]
            prod = prod * jnp.where(par == 0, cost[j], cost_b[j])
            return total + prod.reshape(tiles, 8, LANES).sum(axis=0)

        gamma_part = lax.fori_loop(0, nb, gamma_body, jnp.zeros((8, LANES), jnp.float32))
        acc[1 + layer] = 2.0 * gamma_part
        acc[1 + num_layers + layer] = beta_part
        return 0

    lax.fori_loop(0, num_layers, backward, 0)
    wait_sends((last + 1) % 2 if num_layers == 1 else 1)

    lane = lax.broadcasted_iota(jnp.int32, (1, LANES), 1)
    row = jnp.zeros((1, LANES), jnp.float32)
    for place in range(acc.shape[0]):
        value = jnp.sum(jnp.sum(acc[place], axis=0, keepdims=True), axis=1, keepdims=True)
        row = jnp.where(lane == place, value, row)
    part[...] = row
    for dy, dx, dc in offsets:
        y, x, dest = peer(dy, dx, dc)
        if dy or dx or dc:
            pltpu.make_async_remote_copy(
                src_ref=part, dst_ref=gath.at[me], send_sem=sum_send, recv_sem=sum_recv.at[me],
                device_id={"qy": y, "qx": x}, device_id_type=MESH_ID).start()
        else:
            pltpu.make_async_copy(part, gath.at[me], sum_recv.at[me]).start()

    def sum_wait(j, _):
        pltpu.make_async_copy(part, gath.at[j], sum_recv.at[j]).wait()
        return 0

    lax.fori_loop(0, nb, sum_wait, 0)
    totals[...] = lax.fori_loop(0, nb, lambda j, t: t + gath[j], jnp.zeros((1, LANES), jnp.float32))
    view = gath.at[pl.ds(0, nb - 1)]
    pltpu.make_async_copy(view, view, sum_send).wait()
    view = cost_b.at[pl.ds(0, nb - 1)]
    pltpu.make_async_copy(view, view, cost_send).wait()


def solution(mesh):
    ny, nx = mesh.shape["qy"], mesh.shape["qx"]
    nb = ny * nx

    def local_run(cost_local, gamma_angles, beta_angles):
        chunk = cost_local.shape[0]
        num_layers = gamma_angles.shape[0]
        rows = chunk // (nb * LANES)
        num_qubits = int(math.log2(chunk * nb))
        amp = (chunk * nb) ** -0.5
        vmem, smem = pltpu.VMEM, pltpu.SMEM
        state = (nb, 2, rows, LANES)
        f32 = jnp.float32
        final, totals = pl.pallas_call(
            functools.partial(kernel, ny, nx, num_layers, num_qubits, amp),
            out_shape=(jax.ShapeDtypeStruct((2, nb, rows, LANES), f32), jax.ShapeDtypeStruct((1, LANES), f32)),
            in_specs=[pl.BlockSpec(memory_space=vmem), pl.BlockSpec(memory_space=smem), pl.BlockSpec(memory_space=smem)],
            out_specs=(pl.BlockSpec(memory_space=vmem), pl.BlockSpec(memory_space=vmem)),
            scratch_shapes=[
                vmem((nb, rows, LANES), f32),
                vmem((num_layers, 2, nb, rows, LANES), f32),
                vmem((num_layers,) + state, f32),
                vmem((num_layers,) + state, f32),
                vmem((2,) + state, f32),
                vmem((2,) + state, f32),
                vmem(state, f32),
                vmem(state, f32),
                vmem(state, f32),
                vmem(state, f32),
                vmem((num_layers, 2, 8, LANES), f32),
                vmem((1 + 2 * num_layers, 8, LANES), f32),
                vmem((1, LANES), f32),
                vmem((nb, 1, LANES), f32),
                pltpu.SemaphoreType.DMA((2,)),
                pltpu.SemaphoreType.DMA((2, nb)),
                pltpu.SemaphoreType.DMA,
                pltpu.SemaphoreType.DMA((nb,)),
                pltpu.SemaphoreType.DMA,
                pltpu.SemaphoreType.DMA((nb,)),
            ],
            compiler_params=pltpu.CompilerParams(
                collective_id=0, has_side_effects=True, vmem_limit_bytes=48 * 1024 * 1024),
            name="qaoa",
        )(cost_local.reshape(nb, rows, LANES), gamma_angles, beta_angles)
        energy = totals[0, :1]
        grad = totals[0, 1:1 + 2 * num_layers]
        return energy, grad, final.reshape(2, chunk)

    state_spec = P(("inst", "qy", "qx"))
    return jax.shard_map(
        local_run, mesh=mesh, in_specs=(state_spec, P(), P()),
        out_specs=(P("inst"), P("inst"), P(None, ("inst", "qy", "qx"))), check_vma=False)
```

time: 3030 us -> 225 us (0.07)
  other arithmetic: 1230 us -> 0 us
  waiting for transfers between devices: 791 us -> 0 us
  local copies, waits for them, and re-layouts: 621 us -> 3.38 us
  Pallas kernels: 0 us -> 219 us
  starting transfers between devices: 185 us -> 0 us
  between operations: 135 us -> 1.82 us
  blocking collectives: 44.3 us -> 0 us
    ppermute x80 -> x0, waiting for transfers between devices: 791 us -> none  [partner_block(): lax.ppermute(payload, axis_name, [(position, position ^ mask_bit) for pos...]
    add x182 -> x0, other arithmetic: 344 us -> none  [the longest x128 202 us: mix_qubit(): cos_half * state_vec + sin_half * turn_vec(pair_swap(state_vec, qubit_num))]
    sub x168 -> x0, other arithmetic: 339 us -> none  [the longest x128 294 us: unmix_qubit(): return (cos_half * both_vecs - sin_half * turn_vec(partner), beta_term)]
    slice x467 -> x0, local copies, waits for them, and re-layouts: 321 us -> none  [the longest x192 266 us: turn_vec(): return jnp.stack([state_vec[1], -state_vec[0]])]
    reduce_sum x146 -> x0, other arithmetic: 231 us -> none  [the longest x104 165 us: unmix_qubit(): jnp.sum(both_vecs[0, 1] * partner[1, 0] - both_vecs[1, 1] * partner[0, 0]...]
    pallas_call x0 -> x1, Pallas kernels: none -> 219 us  [local_run(): pl.pallas_call(functools.partial(kernel, ny, nx, num_layers, num_qubits,...]
    unnamed x2220 -> x7, local copies, waits for them, and re-layouts: 213 us -> 2.8 us
    ppermute x80 -> x0, starting transfers between devices: 185 us -> none  [partner_block(): lax.ppermute(payload, axis_name, [(position, position ^ mask_bit) for pos...]
  transfers between devices with their start and end apart: 80 -> 0, of which waited for: 70 -> 0; matrix products, arithmetic and copies ran while one was open for 11% -> 0% of each run, Pallas kernels for 0% -> 0%
where the time goes in v1:
time: 225 us
  Pallas kernels  219 us (97%)
  local copies, waits for them, and re-layouts  3.38 us (2%)
    pallas_call x1, Pallas kernels, local_run(): pl.pallas_call(functools.partial(kernel, ny, nx, num_layers, num_qubits,...  219 us

profile of v1, /device:TPU:97, one launch (start us, length us, event | category | flops | bytes accessed | tf_op | source)
XLA Modules:
  0.0 224.6 jit_solution(5511335593672471067)
XLA Ops:
  0.6 0.0 copy-start.2
  0.6 0.0 copy-start.1
  0.6 0.6 copy-done.2
  1.3 0.0 copy-done.1
  1.3 0.0 copy-start
  1.3 0.9 copy-done
  2.3 219.4 %qaoa.1 = (f32[2,32,16,128]{3,2,1,0:T(8,128)S(1)}, f32[1,128]{1,0:T(1,128)S(1)}) custom-call(f32[32,16,128]{2,1,0:T(8,128)S(1)} %bitcast.11, f32[8]{0:T(128)S(1)} %copy-done.1, f32[8]{0:T(128)S(1)} %copy-done.2), custom_call_target="tpu_custom_call" | custom-call | tf_op jit(solution)/shard_map/qaoa/pallas_call | solution.py:417
  221.6 1.2 copy.8
  222.8 0.6 slice_bitcast_fusion
Async XLA Ops:
  0.6 0.7 copy-start.2
  0.6 0.7 copy-start.1
  1.3 0.9 copy-start

commit v2 on v1

--- a/solution.py
+++ b/solution.py
@@ -44,31 +44,20 @@
     return out
 
 
-def inner_partners(tiles, per_block, apply):
-    lane = lax.broadcasted_iota(jnp.int32, (1, 8, LANES), 2)
-    sub = lax.broadcasted_iota(jnp.int32, (1, 8, LANES), 1)
-
-    def rolled(x, ids, dist, axis, size):
-        if 2 * dist == size:
-            return pltpu.roll(x, dist, axis)
-        upper = (ids // dist) % 2 > 0
-        return jnp.where(upper, pltpu.roll(x, dist, axis), pltpu.roll(x, size - dist, axis))
-
-    for bit in range(7):
-        tiles = apply(tiles, lambda x, d=2 ** bit: rolled(x, lane, d, 2, LANES))
-    for bit in range(3):
-        tiles = apply(tiles, lambda x, d=2 ** bit: rolled(x, sub, d, 1, 8))
-    stride = 1
-    while stride < per_block:
-        def swapped(x, d=stride):
-            return jnp.concatenate([x[(i ^ d):(i ^ d) + 1] for i in range(x.shape[0])], axis=0)
-        tiles = apply(tiles, swapped)
-        stride *= 2
-    return tiles
+def sublane_partner(x, ids, dist):
+    return jnp.take_along_axis(x, ids ^ dist, axis=0, mode="promise_in_bounds")
+
+
+def rows_of(tiles):
+    return jnp.concatenate(tiles, axis=0)
+
+
+def matmul(x, w):
+    return jnp.dot(x, w, precision=lax.Precision.HIGHEST, preferred_element_type=jnp.float32)
 
 
 def kernel(ny, nx, num_layers, num_qubits, amp, cost, gamma, beta, final, totals,
-           cost_b, tabs, post, pre, recv, send, work, lam, lam_pre, qbuf, angle, acc, part, gath,
+           cost_b, tabs, post, pre, recv, send, work, lam, lam_pre, qbuf, angle, lane_mix, lane_sum, acc, part, gath,
            send_sem, recv_sem, cost_send, cost_recv, sum_send, sum_recv):
     nb = ny * nx
     chips = nx // 2
@@ -94,16 +83,42 @@
             y, x, _ = peer(dy, dx, dc)
             pl.semaphore_signal(barrier, inc=1, device_id={"qy": y, "qx": x}, device_id_type=MESH_ID)
 
+    flips = lax.broadcasted_iota(jnp.int32, (LANES, LANES), 0) ^ lax.broadcasted_iota(jnp.int32, (LANES, LANES), 1)
+    weight = sum((flips >> bit) & 1 for bit in range(7))
+    ones = jnp.where(weight == 1, 1.0, 0.0).astype(jnp.float32)
+    lane_sum[:LANES, :LANES] = ones
+    lane_sum[LANES:, LANES:] = ones
+    lane_sum[:LANES, LANES:] = jnp.zeros_like(ones)
+    lane_sum[LANES:, :LANES] = jnp.zeros_like(ones)
     for layer in range(num_layers):
         half = jnp.full((8, LANES), 0.5 * beta[layer], jnp.float32)
         cos_half, sin_half = jnp.cos(half), jnp.sin(half)
-        scale, power, left = None, cos_half, num_qubits
+        scale, power, left = None, cos_half, num_qubits - 7
         while left:
             if left % 2:
                 scale = power if scale is None else scale * power
             power, left = power * power, left // 2
         angle[layer, 0] = sin_half / cos_half
         angle[layer, 1] = scale
+        coefs = []
+        for k in range(8):
+            c = cos_half[:1]
+            s = sin_half[:1]
+            coef = None
+            for factor in [c] * (7 - k) + [s] * k:
+                coef = factor if coef is None else coef * factor
+            coefs.append(coef)
+        even, odd = jnp.zeros((LANES, LANES), jnp.float32), jnp.zeros((LANES, LANES), jnp.float32)
+        for k in range(8):
+            value = coefs[k] if (k // 2) % 2 == 0 else -coefs[k]
+            if k % 2 == 0:
+                even = jnp.where(weight == k, value, even)
+            else:
+                odd = jnp.where(weight == k, value, odd)
+        lane_mix[layer, :LANES, :LANES] = even
+        lane_mix[layer, LANES:, LANES:] = even
+        lane_mix[layer, LANES:, :LANES] = odd
+        lane_mix[layer, :LANES, LANES:] = -odd
 
     def angle_of(layer, kind):
         tile = angle[layer, kind]
@@ -153,35 +168,36 @@
                 for dc in (1, 0):
                     start_send(par, dy, dx, dc)
 
-    groups = (nb + 3) // 4
-
-    def receive(par, tan_half):
-        tile = tan_half[:8].reshape(1, 8, LANES)
+    sub = lax.broadcasted_iota(jnp.int32, (8, LANES), 0)
+
+    def load_row(ref, y):
+        return [(ref[y * nx + x, 0, 8 * i:8 * i + 8], ref[y * nx + x, 1, 8 * i:8 * i + 8])
+                for x in range(nx) for i in range(tiles)]
+
+    def receive(par, layer, tan_half, back):
+        tan_tile = tan_half[:8]
 
         def body(i, _):
-            slots = []
-            for k in range(nb // groups):
-                n = i * (nb // groups) + k
-                dy = (n // nx + ny // 2) % ny
-                dx = ((n % nx) // 2 + chips // 2) % chips
-                _, _, slot = peer(dy, dx, n % 2)
-                view = recv.at[par, slot]
-                pltpu.make_async_copy(view, view, recv_sem.at[par, slot]).wait()
-                slots.append(slot)
-            re = jnp.concatenate([recv[par, s, 0].reshape(tiles, 8, LANES) for s in slots], axis=0)
-            im = jnp.concatenate([recv[par, s, 1].reshape(tiles, 8, LANES) for s in slots], axis=0)
-            re, im = inner_partners((re, im), tiles, lambda t, f: (t[0] + tile * f(t[1]), t[1] - tile * f(t[0])))
-            for k, s in enumerate(slots):
-                recv[par, s, 0] = re[k * tiles:(k + 1) * tiles].reshape(rows, LANES)
-                recv[par, s, 1] = im[k * tiles:(k + 1) * tiles].reshape(rows, LANES)
+            y = (my_y + i + ny // 2) % ny
+            for dx in range(chips):
+                for dc in range(2):
+                    slot = y * nx + ((my_chip + chips // 2 + dx) % chips) * 2 + (my_core + dc) % 2
+                    view = recv.at[par, slot]
+                    pltpu.make_async_copy(view, view, recv_sem.at[par, slot]).wait()
+            row = load_row(recv.at[par], y)
+            for dist in (1, 2, 4):
+                row = [(re + tan_tile * sublane_partner(im, sub, dist), im - tan_tile * sublane_partner(re, sub, dist))
+                       for re, im in row]
+            row = mix_all(row, tan_tile)
+            re, im = rows_of([t[0] for t in row]), rows_of([t[1] for t in row])
+            mixed = matmul(jnp.concatenate([im, re] if back else [re, im], axis=1), lane_mix[layer])
+            first, second = mixed[:, :LANES], mixed[:, LANES:]
+            re, im = (second, first) if back else (first, second)
+            for x in range(nx):
+                work[y * nx + x, 0] = re[x * rows:(x + 1) * rows]
+                work[y * nx + x, 1] = im[x * rows:(x + 1) * rows]
             return 0
 
-        lax.fori_loop(0, groups, body, 0)
-
-    def all_low_bits(par, tan_half):
-        def body(y, _):
-            low_bits(recv.at[par], work, tan_half, y)
-            return 0
         lax.fori_loop(0, ny, body, 0)
 
     def column(x):
@@ -246,8 +262,7 @@
 
         tan_half, scale = angle_of(layer, 0), angle_of(layer, 1)
         tan_next = angle_of(layer + 1, 0)
-        receive(par, tan_half)
-        all_low_bits(par, tan_half)
+        receive(par, layer, tan_half, False)
 
         def middle(places):
             blocks = scaled(mix_all(load(work, places), tan_half), scale)
@@ -270,8 +285,7 @@
     last = num_layers - 1
     par = last % 2
     tan_half, scale = angle_of(last, 0), angle_of(last, 1)
-    receive(par, tan_half)
-    all_low_bits(par, tan_half)
+    receive(par, last, tan_half, False)
     root = jnp.float32(1.0 / amp)
 
     def turn_point(places):
@@ -296,10 +310,24 @@
     def im_dot(left, right):
         return (left[0] * right[1] - left[1] * right[0]).reshape(tiles, 8, LANES).sum(axis=0)
 
-    def block_sums(src):
+    def block_sums(src, inner):
         def low(y, _):
-            places = [y * nx + x for x in range(nx)]
-            store(qbuf, places, partner_sums(load(src, places)))
+            row = load_row(src, y)
+            if inner:
+                re, im = rows_of([t[0] for t in row]), rows_of([t[1] for t in row])
+                lanes = matmul(jnp.concatenate([re, im], axis=1), lane_sum[...])
+                total = partner_sums(row)
+                for n, (re, im) in enumerate(row):
+                    sre, sim = total[n]
+                    for dist in (1, 2, 4):
+                        sre += sublane_partner(re, sub, dist)
+                        sim += sublane_partner(im, sub, dist)
+                    place, top = y * nx + n // tiles, 8 * (n % tiles)
+                    qbuf[place, 0, top:top + 8] = sre + lanes[8 * n:8 * n + 8, :LANES]
+                    qbuf[place, 1, top:top + 8] = sim + lanes[8 * n:8 * n + 8, LANES:]
+            else:
+                places = [y * nx + x for x in range(nx)]
+                store(qbuf, places, partner_sums(load(src, places)))
             return 0
 
         lax.fori_loop(0, ny, low, 0)
@@ -309,20 +337,6 @@
             store(qbuf, places, [(a + c, b + d) for (a, b), (c, d) in zip(sums, load(qbuf, places))])
 
         for_columns(high)
-
-    def inner_sums(src):
-        def body(j, _):
-            x = (src[j, 0].reshape(tiles, 8, LANES), src[j, 1].reshape(tiles, 8, LANES))
-            total = (qbuf[j, 0].reshape(tiles, 8, LANES), qbuf[j, 1].reshape(tiles, 8, LANES))
-            parts = []
-            inner_partners(x, tiles, lambda t, f: (parts.append((f(t[0]), f(t[1]))), t)[1])
-            for re, im in parts:
-                total = (total[0] + re, total[1] + im)
-            qbuf[j, 0] = total[0].reshape(rows, LANES)
-            qbuf[j, 1] = total[1].reshape(rows, LANES)
-            return 0
-
-        lax.fori_loop(0, nb, body, 0)
 
     def dot_with_sums(left):
         def body(j, total):
@@ -333,14 +347,12 @@
         layer = last - step
         par = layer % 2
         back = 1 - par
-        block_sums(post.at[layer])
+        block_sums(post.at[layer], False)
         beta_part = dot_with_sums(lam)
-        block_sums(pre.at[layer])
-        inner_sums(pre.at[layer])
+        block_sums(pre.at[layer], True)
 
         tan_half, scale = -angle_of(layer, 0), angle_of(layer, 1)
-        receive(back, tan_half)
-        all_low_bits(back, tan_half)
+        receive(back, layer, tan_half, True)
 
         before = lax.max(layer - 1, 0)
         tan_next = -angle_of(before, 0)
@@ -431,6 +443,8 @@
                 vmem(state, f32),
                 vmem(state, f32),
                 vmem((num_layers, 2, 8, LANES), f32),
+                vmem((num_layers, 2 * LANES, 2 * LANES), f32),
+                vmem((2 * LANES, 2 * LANES), f32),
                 vmem((1 + 2 * num_layers, 8, LANES), f32),
                 vmem((1, LANES), f32),
                 vmem((nb, 1, LANES), f32),

time: 225 us -> 182 us (0.81)
  Pallas kernels: 219 us -> 177 us
    pallas_call x1, Pallas kernels: 219 us -> 177 us  [local_run(): pl.pallas_call(functools.partial(kernel, ny, nx, num_layers, num_qubits,...]
where the time goes in v2:
time: 182 us
  Pallas kernels  177 us (97%)
  local copies, waits for them, and re-layouts  3.38 us (2%)
  between operations  1.82 us (1%)
    pallas_call x1, Pallas kernels, local_run(): pl.pallas_call(functools.partial(kernel, ny, nx, num_layers, num_qubits,...  177 us

profile of v2, /device:TPU:97, one launch (start us, length us, event | category | flops | bytes accessed | tf_op | source)
XLA Modules:
  0.0 181.8 jit_solution(7901589162849370568)
XLA Ops:
  0.6 0.0 copy-start.2
  0.6 0.0 copy-start.1
  0.6 0.6 copy-done.2
  1.3 0.0 copy-done.1
  1.3 0.0 copy-start
  1.3 0.9 copy-done
  2.3 176.6 %qaoa.1 = (f32[2,32,16,128]{3,2,1,0:T(8,128)S(1)}, f32[1,128]{1,0:T(1,128)S(1)}) custom-call(f32[32,16,128]{2,1,0:T(8,128)S(1)} %bitcast.11, f32[8]{0:T(128)S(1)} %copy-done.1, f32[8]{0:T(128)S(1)} %copy-done.2), custom_call_target="tpu_custom_call" | custom-call | tf_op jit(solution)/shard_map/qaoa/pallas_call | solution.py:429
  178.9 1.2 copy.8
  180.1 0.6 slice_bitcast_fusion
Async XLA Ops:
  0.6 0.7 copy-start.2
  0.6 0.7 copy-start.1
  1.3 0.9 copy-start

commit v3 on v0

v3 whole, which is shorter than its diff:
```python
import functools
import math

import jax
import jax.numpy as jnp
from jax import lax
from jax.experimental import pallas as pl
from jax.experimental.pallas import tpu as pltpu
from jax.sharding import PartitionSpec as P

LANES = 128
MESH_ID = pl.DeviceIdType.MESH


def mix_pair(blocks, tan_half, stride):
    out = list(blocks)
    for low in range(len(blocks)):
        if low & stride:
            continue
        high = low | stride
        (re0, im0), (re1, im1) = blocks[low], blocks[high]
        out[low] = (re0 + tan_half * im1, im0 - tan_half * re1)
        out[high] = (re1 + tan_half * im0, im1 - tan_half * re0)
    return out


def mix_all(blocks, tan_half):
    stride = 1
    while stride < len(blocks):
        blocks = mix_pair(blocks, tan_half, stride)
        stride *= 2
    return blocks


def partner_sums(blocks):
    out = []
    for place in range(len(blocks)):
        stride, re, im = 1, None, None
        while stride < len(blocks):
            pre, pim = blocks[place ^ stride]
            re, im = (pre, pim) if re is None else (re + pre, im + pim)
            stride *= 2
        out.append((re, im))
    return out


def sublane_partner(x, ids, dist):
    return jnp.take_along_axis(x, ids ^ dist, axis=1, mode="promise_in_bounds")


def swapped(x, stride):
    pairs = x.reshape((x.shape[0] // (2 * stride), 2, stride) + x.shape[1:])
    return jnp.concatenate([pairs[:, 1:], pairs[:, :1]], axis=1).reshape(x.shape)


def mix_leading(re, im, tan_half, size):
    stride = 1
    while stride < size:
        re, im = re + tan_half * swapped(im, stride), im - tan_half * swapped(re, stride)
        stride *= 2
    return re, im


def matmul(x, w):
    return jnp.dot(x, w, precision=lax.Precision.HIGHEST, preferred_element_type=jnp.float32)


def kernel(ny, nx, num_layers, num_qubits, amp, cost, gamma, beta, final, totals,
           cost_b, tabs, kept, recv, send, work, qbuf, angle, lane_mix, lane_sum, acc, part, gath,
           send_sem, recv_sem, cost_send, cost_recv, sum_send, sum_recv):
    nb = ny * nx
    chips = nx // 2
    last = num_layers - 1
    my_y = lax.axis_index("qy")
    my_x = lax.axis_index("qx")
    my_chip, my_core = my_x // 2, my_x % 2
    me = my_y * nx + my_x

    def peer(dy, dx, dc):
        y = (my_y + dy) % ny
        x = ((my_chip + dx) % chips) * 2 + (my_core + dc) % 2
        return y, x, y * nx + x

    dy_order = sorted(range(ny), key=lambda d: -min(d, ny - d))
    dx_order = sorted(range(chips), key=lambda d: -min(d, chips - d))
    offsets = [(dy, dx, dc) for dy in dy_order for dx in dx_order for dc in (1, 0) if dy or dx or dc]

    barrier = pltpu.get_barrier_semaphore()
    for dy, dx, dc in offsets:
        y, x, _ = peer(dy, dx, dc)
        pl.semaphore_signal(barrier, inc=1, device_id={"qy": y, "qx": x}, device_id_type=MESH_ID)

    def make_angle(layer):
        half = jnp.full((8, LANES), 0.5 * beta[layer], jnp.float32)
        cos_half, sin_half = jnp.cos(half), jnp.sin(half)
        scale, power, left = None, cos_half, num_qubits - 7
        while left:
            if left % 2:
                scale = power if scale is None else scale * power
            power, left = power * power, left // 2
        angle[layer, 0] = sin_half / cos_half
        angle[layer, 1] = scale
        return cos_half[:1], sin_half[:1]

    def make_lanes():
        flips = lax.broadcasted_iota(jnp.int32, (LANES, LANES), 0) ^ lax.broadcasted_iota(jnp.int32, (LANES, LANES), 1)
        weight = sum((flips >> bit) & 1 for bit in range(7))
        ones = jnp.where(weight == 1, 1.0, 0.0).astype(jnp.float32)
        lane_sum[:LANES, :LANES] = ones
        lane_sum[LANES:, LANES:] = ones
        lane_sum[:LANES, LANES:] = jnp.zeros_like(ones)
        lane_sum[LANES:, :LANES] = jnp.zeros_like(ones)
        for layer in range(num_layers):
            c, s = make_angle(layer)
            coefs = []
            for k in range(8):
                coef = None
                for factor in [c] * (7 - k) + [s] * k:
                    coef = factor if coef is None else coef * factor
                coefs.append(coef if (k // 2) % 2 == 0 else -coef)
            even, odd = jnp.zeros((LANES, LANES), jnp.float32), jnp.zeros((LANES, LANES), jnp.float32)
            for k in range(8):
                if k % 2 == 0:
                    even = jnp.where(weight == k, coefs[k], even)
                else:
                    odd = jnp.where(weight == k, coefs[k], odd)
            lane_mix[layer, :LANES, :LANES] = even
            lane_mix[layer, LANES:, LANES:] = even
            lane_mix[layer, LANES:, :LANES] = odd
            lane_mix[layer, :LANES, LANES:] = -odd

    def make_table(layer, source):
        g = gamma[layer]

        def body(j, _):
            for h in range(2):
                theta = g * source[j, h]
                tabs[layer, 0, h, j] = jnp.cos(theta)
                tabs[layer, 1, h, j] = jnp.sin(theta)
            return 0

        lax.fori_loop(0, nb, body, 0)

    def load(ref, places):
        return [(ref[h, j, 0], ref[h, j, 1]) for h, j in places]

    def store(ref, places, blocks):
        for (h, j), (re, im) in zip(places, blocks):
            ref[h, j, 0] = re
            ref[h, j, 1] = im

    def turn(blocks, layer, places):
        out = []
        for (re, im), (h, j) in zip(blocks, places):
            c, s = tabs[layer, 0, h, j], tabs[layer, 1, h, j]
            out.append((c * re + s * im, c * im - s * re))
        return out

    def scaled(blocks, scale):
        return [(scale * re, scale * im) for re, im in blocks]

    def column(x, halves):
        return [(h, y * nx + x) for y in range(ny) for h in halves]

    def for_columns(halves, body):
        lax.fori_loop(0, nx, lambda x, _: (body(column(x, halves)), 0)[1], 0)

    def load_row(ref, h, y):
        return ref[h, pl.ds(y * nx, nx), 0], ref[h, pl.ds(y * nx, nx), 1]

    def store_row(ref, h, y, row):
        for c in range(2):
            ref[h, pl.ds(y * nx, nx), c] = row[c]

    def send_half(par, h, tan_half):
        for dy in dy_order:
            y = (my_y + dy) % ny
            re, im = load_row(work, h, y)
            store_row(send.at[par], h, y, mix_leading(re, im, tan_half, nx))
            for dx in dx_order:
                for dc in (1, 0):
                    if dy or dx or dc:
                        _, x, dest = peer(dy, dx, dc)
                        pltpu.make_async_remote_copy(
                            src_ref=send.at[par, h, dest], dst_ref=recv.at[par, h, me],
                            send_sem=send_sem.at[par, h], recv_sem=recv_sem.at[par, h, me],
                            device_id={"qy": y, "qx": x}, device_id_type=MESH_ID).start()
        for c in range(2):
            recv[par, h, me, c] = send[par, h, me, c]

    def wait_sends(par, h):
        view = send.at[par, h, pl.ds(0, nb - 1)]
        pltpu.make_async_copy(view, view, send_sem.at[par, h]).wait()

    sub = lax.broadcasted_iota(jnp.int32, (nx, 8, LANES), 1)
    source_order = [(ny - dy) % ny for dy in dy_order]
    waves = [source_order[i:i + 2] for i in range(0, ny, 2)]

    def receive(par, h, layer, tan_half):
        for wave in waves:
            rows = []
            for dy in wave:
                y = (my_y + dy) % ny
                for dx in dx_order:
                    for dc in (1, 0):
                        if dy or dx or dc:
                            slot = peer(dy, dx, dc)[2]
                            view = recv.at[par, h, slot]
                            pltpu.make_async_copy(view, view, recv_sem.at[par, h, slot]).wait()
                re, im = load_row(recv.at[par], h, y)
                for dist in (1, 2, 4):
                    re, im = (re + tan_half * sublane_partner(im, sub, dist),
                              im - tan_half * sublane_partner(re, sub, dist))
                re, im = mix_leading(re, im, tan_half, nx)
                rows.append(jnp.concatenate([re.reshape(nx * 8, LANES), im.reshape(nx * 8, LANES)], axis=1))
            mixed = matmul(jnp.concatenate(rows, axis=0), lane_mix[layer])
            for k, dy in enumerate(wave):
                part_rows = mixed[k * nx * 8:(k + 1) * nx * 8]
                store_row(work, h, (my_y + dy) % ny, (part_rows[:, :LANES].reshape(nx, 8, LANES),
                                                      part_rows[:, LANES:].reshape(nx, 8, LANES)))

    def per_half(body):
        lax.fori_loop(0, 2, lambda h, _: (body(h), 0)[1], 0)

    make_angle(0)
    make_table(0, cost)
    tan0 = angle[0, 0]

    def first(places):
        flat = jnp.full((8, LANES), amp, jnp.float32)
        blocks = turn([(flat, jnp.zeros_like(flat)) for _ in places], 0, places)
        store(kept.at[num_layers], places, blocks)
        store(work, places, mix_all(blocks, tan0))

    for_columns((0, 1), first)
    for place in range(acc.shape[0]):
        acc[place] = jnp.zeros((8, LANES), jnp.float32)

    pl.semaphore_wait(barrier, nb - 1)

    for dy, dx, dc in offsets:
        y, x, dest = peer(dy, dx, dc)
        pltpu.make_async_remote_copy(
            src_ref=cost.at[dest], dst_ref=cost_b.at[me], send_sem=cost_send, recv_sem=cost_recv.at[me],
            device_id={"qy": y, "qx": x}, device_id_type=MESH_ID).start()
    for h in range(2):
        cost_b[me, h] = cost[me, h]
    per_half(lambda h: send_half(0, h, tan0))
    make_lanes()
    for dy, dx, dc in offsets:
        slot = peer(dy, dx, dc)[2]
        pltpu.make_async_copy(cost_b.at[slot], cost_b.at[slot], cost_recv.at[slot]).wait()
    make_table(1, cost_b)

    before_at, lam_pre, lam = num_layers, 2 * num_layers, 2 * num_layers + 1
    root = jnp.float32(1.0 / amp)
    zero = jnp.zeros((8, LANES), jnp.float32)
    pairs = num_layers // 2

    def plan(step):
        back = step // num_layers
        done = step + back * (2 * num_layers - 1 - 2 * step)
        return back, done, done + 1 - back, (done + 1 - 2 * back + num_layers) % num_layers

    def middle(step):
        back, done, turned, following = plan(step)
        tan_half, scale, tan_next = angle[done, 0], angle[done, 1], angle[following, 0]
        first_at = done + back * (lam_pre - done)
        second_at = before_at + turned + back * (lam - before_at - turned)

        def body(places):
            blocks = scaled(mix_all(load(work, places), tan_half), scale)
            store(kept.at[first_at], places, blocks)
            blocks = turn(blocks, turned, places)
            store(kept.at[second_at], places, blocks)
            store(work, places, mix_all(blocks, tan_next))

        return body

    def turn_point(places):
        tan_half, scale = angle[last, 0], angle[last, 1]
        blocks = scaled(mix_all(load(work, places), tan_half), scale)
        store(kept.at[last], places, blocks)
        conj = []
        energy = acc[0]
        for (h, j), (re, im) in zip(places, blocks):
            c = cost[j, h]
            final[0, j, h] = root * re
            final[1, j, h] = root * im
            conj.append((c * re, -(c * im)))
            energy += c * (re * re + im * im)
        acc[0] = energy
        store(kept.at[lam], places, conj)
        store(work, places, mix_all(conj, tan_half))

    def im_dot(conj, right):
        return conj[0] * right[1] + conj[1] * right[0]

    def sums_of(re, im, size):
        total_re, total_im, stride = swapped(re, 1), swapped(im, 1), 2
        while stride < size:
            total_re, total_im, stride = total_re + swapped(re, stride), total_im + swapped(im, stride), 2 * stride
        return total_re, total_im

    def high_sums(at):
        def body(x, _):
            for h in range(2):
                places = column(x, (h,))
                sums = partner_sums(load(kept.at[at], places))
                store(qbuf, places, [(a + c, b + d) for (a, b), (c, d) in zip(sums, load(qbuf, places))])
            return 0

        lax.fori_loop(0, nx, body, 0)

    def prepare(layer):
        def low(n, _):
            h, y = n // ny, n % ny
            re, im = load_row(kept.at[layer], h, y)
            store_row(qbuf, h, y, sums_of(re, im, nx))
            return 0

        lax.fori_loop(0, 2 * ny, low, 0)
        high_sums(layer)

        def body(j, total):
            for h in range(2):
                total += im_dot((kept[lam, h, j, 0], kept[lam, h, j, 1]), (qbuf[h, j, 0], qbuf[h, j, 1]))
            return total

        acc[1 + num_layers + layer] = lax.fori_loop(0, nb, body, zero)
        at = before_at + layer

        def inner(y, _):
            rows = [load_row(kept.at[at], h, y) for h in range(2)]
            x = jnp.concatenate([jnp.concatenate([re.reshape(nx * 8, LANES), im.reshape(nx * 8, LANES)], axis=1)
                                 for re, im in rows], axis=0)
            lanes = matmul(x, lane_sum[...])
            for h in range(2):
                sre, sim = sums_of(*rows[h], nx)
                (re, im), (ore, oim) = rows[h], rows[1 - h]
                for dist in (1, 2, 4):
                    sre += sublane_partner(re, sub, dist)
                    sim += sublane_partner(im, sub, dist)
                mine = lanes[h * nx * 8:(h + 1) * nx * 8]
                store_row(qbuf, h, y, (sre + ore + mine[:, :LANES].reshape(nx, 8, LANES),
                                       sim + oim + mine[:, LANES:].reshape(nx, 8, LANES)))
            return 0

        lax.fori_loop(0, ny, inner, 0)
        high_sums(at)

    def collect(layer, source):
        at = before_at + layer

        def body(j, sums):
            gamma_sum, beta_sum = sums
            for h in range(2):
                left = (kept[lam_pre, h, j, 0], kept[lam_pre, h, j, 1])
                gamma_sum += source[j, h] * im_dot(left, (kept[at, h, j, 0], kept[at, h, j, 1]))
                beta_sum += im_dot(left, (qbuf[h, j, 0], qbuf[h, j, 1]))
            return gamma_sum, beta_sum

        gamma_sum, beta_sum = lax.fori_loop(0, nb, body, (zero, zero))
        acc[1 + layer] = 2.0 * gamma_sum
        acc[1 + num_layers + layer] += beta_sum

    def last_sums(x, sums):
        gamma_sum, beta_sum = sums
        places = column(x, (0, 1))
        blocks = scaled(mix_all(load(work, places), angle[0, 0]), angle[0, 1])
        for (h, j), left, right, q in zip(places, blocks, load(kept.at[before_at], places), load(qbuf, places)):
            gamma_sum += cost[j, h] * im_dot(left, right)
            beta_sum += im_dot(left, q)
        return gamma_sum, beta_sum

    def two_gaps(k, _):
        step = 2 * k
        _, done, _, following = plan(step)
        tan_half, tan_next = angle[done, 0], angle[following, 0]

        def half(h):
            receive(0, h, done, tan_half)
            for_columns((h,), middle(step))

            @pl.when(k > 0)
            def _():
                wait_sends(1, h)

            send_half(1, h, tan_next)

        per_half(half)

        @pl.when(k < pairs - 1)
        def _():
            make_table(step + 2, cost)

        @pl.when(k >= pairs)
        def _():
            collect(done, cost_b)
            prepare(following)

        step = 2 * k + 1
        _, done, _, following = plan(step)
        tan_half = angle[done, 0]
        per_half(lambda h: receive(1, h, done, tan_half))

        @pl.when(k % pairs < pairs - 1)
        def _():
            for_columns((0, 1), middle(step))

        @pl.when(k == pairs - 1)
        def _():
            for_columns((0, 1), turn_point)

        @pl.when(k < 2 * pairs - 1)
        def _():
            tan_next = angle[following - (k // (pairs - 1)) * (1 - k // pairs) * (following - last), 0]

            def half_joint(h):
                wait_sends(0, h)
                send_half(0, h, tan_next)

            per_half(half_joint)

        @pl.when(k < pairs - 1)
        def _():
            make_table(step + 2, cost_b)

        @pl.when((k >= pairs) & (k < 2 * pairs - 1))
        def _():
            collect(done, cost)

        @pl.when((k >= pairs - 1) & (k < 2 * pairs - 1))
        def _():
            prepare(2 * num_layers - 3 - 2 * k)

        return 0

    lax.fori_loop(0, 2 * pairs, two_gaps, 0)
    gamma_sum, beta_sum = lax.fori_loop(0, nx, last_sums, (zero, zero))
    acc[1] = 2.0 * gamma_sum
    acc[1 + num_layers] += beta_sum

    lane = lax.broadcasted_iota(jnp.int32, (1, LANES), 1)
    row = jnp.zeros((1, LANES), jnp.float32)
    for place in range(acc.shape[0]):
        value = jnp.sum(jnp.sum(acc[place], axis=0, keepdims=True), axis=1, keepdims=True)
        row = jnp.where(lane == place, value, row)
    part[...] = row
    for dy, dx, dc in offsets:
        y, x, dest = peer(dy, dx, dc)
        pltpu.make_async_remote_copy(
            src_ref=part, dst_ref=gath.at[me], send_sem=sum_send, recv_sem=sum_recv.at[me],
            device_id={"qy": y, "qx": x}, device_id_type=MESH_ID).start()
    gath[me] = row
    for par in range(2):
        for h in range(2):
            wait_sends(par, h)
    view = cost_b.at[pl.ds(0, nb - 1)]
    pltpu.make_async_copy(view, view, cost_send).wait()
    for dy, dx, dc in offsets:
        slot = peer(dy, dx, dc)[2]
        pltpu.make_async_copy(part, gath.at[slot], sum_recv.at[slot]).wait()
    total = gath[0]
    for j in range(1, nb):
        total += gath[j]
    totals[...] = total
    view = gath.at[pl.ds(0, nb - 1)]
    pltpu.make_async_copy(view, view, sum_send).wait()


def solution(mesh):
    ny, nx = mesh.shape["qy"], mesh.shape["qx"]
    nb = ny * nx

    def local_run(cost_local, gamma_angles, beta_angles):
        chunk = cost_local.shape[0]
        num_layers = gamma_angles.shape[0]
        assert chunk == nb * 16 * LANES and num_layers % 2 == 0
        num_qubits = int(math.log2(chunk * nb))
        amp = (chunk * nb) ** -0.5
        vmem, smem, dma = pltpu.VMEM, pltpu.SMEM, pltpu.SemaphoreType.DMA
        f32 = jnp.float32
        state = (2, nb, 2, 8, LANES)
        final, totals = pl.pallas_call(
            functools.partial(kernel, ny, nx, num_layers, num_qubits, amp),
            out_shape=(jax.ShapeDtypeStruct((2, nb, 2, 8, LANES), f32), jax.ShapeDtypeStruct((1, LANES), f32)),
            in_specs=[pl.BlockSpec(memory_space=vmem), pl.BlockSpec(memory_space=smem), pl.BlockSpec(memory_space=smem)],
            out_specs=(pl.BlockSpec(memory_space=vmem), pl.BlockSpec(memory_space=vmem)),
            scratch_shapes=[
                vmem((nb, 2, 8, LANES), f32),
                vmem((num_layers, 2, 2, nb, 8, LANES), f32),
                vmem((2 * num_layers + 2,) + state, f32),
                vmem((2,) + state, f32),
                vmem((2,) + state, f32),
                vmem(state, f32),
                vmem(state, f32),
                vmem((num_layers, 2, 8, LANES), f32),
                vmem((num_layers, 2 * LANES, 2 * LANES), f32),
                vmem((2 * LANES, 2 * LANES), f32),
                vmem((1 + 2 * num_layers, 8, LANES), f32),
                vmem((1, LANES), f32),
                vmem((nb, 1, LANES), f32),
                dma((2, 2)),
                dma((2, 2, nb)),
                dma,
                dma((nb,)),
                dma,
                dma((nb,)),
            ],
            compiler_params=pltpu.CompilerParams(
                collective_id=0, has_side_effects=True, vmem_limit_bytes=48 * 1024 * 1024),
            name="qaoa",
        )(cost_local.reshape(nb, 2, 8, LANES), gamma_angles, beta_angles)
        energy = totals[0, :1]
        grad = totals[0, 1:1 + 2 * num_layers]
        return energy, grad, final.reshape(2, chunk)

    state_spec = P(("inst", "qy", "qx"))
    return jax.shard_map(
        local_run, mesh=mesh, in_specs=(state_spec, P(), P()),
        out_specs=(P("inst"), P("inst"), P(None, ("inst", "qy", "qx"))), check_vma=False)
```

time: 3030 us -> 165 us (0.05)
  other arithmetic: 1230 us -> 0 us
  waiting for transfers between devices: 791 us -> 0 us
  local copies, waits for them, and re-layouts: 621 us -> 3.38 us
  starting transfers between devices: 185 us -> 0 us
  Pallas kernels: 0 us -> 160 us
  between operations: 135 us -> 1.82 us
  blocking collectives: 44.3 us -> 0 us
    ppermute x80 -> x0, waiting for transfers between devices: 791 us -> none  [partner_block(): lax.ppermute(payload, axis_name, [(position, position ^ mask_bit) for pos...]
    add x182 -> x0, other arithmetic: 344 us -> none  [the longest x128 202 us: mix_qubit(): cos_half * state_vec + sin_half * turn_vec(pair_swap(state_vec, qubit_num))]
    sub x168 -> x0, other arithmetic: 339 us -> none  [the longest x128 294 us: unmix_qubit(): return (cos_half * both_vecs - sin_half * turn_vec(partner), beta_term)]
    slice x467 -> x0, local copies, waits for them, and re-layouts: 321 us -> none  [the longest x192 266 us: turn_vec(): return jnp.stack([state_vec[1], -state_vec[0]])]
    reduce_sum x146 -> x0, other arithmetic: 231 us -> none  [the longest x104 165 us: unmix_qubit(): jnp.sum(both_vecs[0, 1] * partner[1, 0] - both_vecs[1, 1] * partner[0, 0]...]
    unnamed x2220 -> x7, local copies, waits for them, and re-layouts: 213 us -> 2.8 us
    ppermute x80 -> x0, starting transfers between devices: 185 us -> none  [partner_block(): lax.ppermute(payload, axis_name, [(position, position ^ mask_bit) for pos...]
    pallas_call x0 -> x1, Pallas kernels: none -> 160 us  [local_run(): pl.pallas_call(functools.partial(kernel, ny, nx, num_layers, num_qubits,...]
  transfers between devices with their start and end apart: 80 -> 0, of which waited for: 70 -> 0; matrix products, arithmetic and copies ran while one was open for 11% -> 0% of each run, Pallas kernels for 0% -> 0%
where the time goes in v3:
time: 165 us
  Pallas kernels  160 us (97%)
  local copies, waits for them, and re-layouts  3.38 us (2%)
  between operations  1.82 us (1%)
    pallas_call x1, Pallas kernels, local_run(): pl.pallas_call(functools.partial(kernel, ny, nx, num_layers, num_qubits,...  160 us

profile of v3, /device:TPU:97, one launch (start us, length us, event | category | flops | bytes accessed | tf_op | source)
XLA Modules:
  0.0 165.0 jit_solution(9926163810357408358)
XLA Ops:
  0.6 0.0 copy-start.2
  0.6 0.0 copy-start.1
  0.6 0.6 copy-done.2
  1.3 0.0 copy-done.1
  1.3 0.0 copy-start
  1.3 0.9 copy-done
  2.3 159.8 %qaoa.1 = (f32[2,32,2,8,128]{4,3,2,1,0:T(8,128)S(1)}, f32[1,128]{1,0:T(1,128)S(1)}) custom-call(f32[32,2,8,128]{3,2,1,0:T(8,128)S(1)} %bitcast.11, f32[8]{0:T(128)S(1)} %copy-done.1, f32[8]{0:T(128)S(1)} %copy-done.2), custom_call_target="tpu_custom_call" | custom-call | tf_op jit(solution)/shard_map/qaoa/pallas_call | solution.py:485
  162.1 1.2 copy.8
  163.3 0.6 slice_bitcast_fusion
Async XLA Ops:
  0.6 0.7 copy-start.2
  0.6 0.7 copy-start.1
  1.3 0.9 copy-start

commit v4 on v3

--- a/solution.py
+++ b/solution.py
@@ -65,9 +65,9 @@
     return jnp.dot(x, w, precision=lax.Precision.HIGHEST, preferred_element_type=jnp.float32)
 
 
-def kernel(ny, nx, num_layers, num_qubits, amp, cost, gamma, beta, final, totals,
-           cost_b, tabs, kept, recv, send, work, qbuf, angle, lane_mix, lane_sum, acc, part, gath,
-           send_sem, recv_sem, cost_send, cost_recv, sum_send, sum_recv):
+def kernel(ny, nx, num_layers, num_qubits, amp, cost_in, gamma_in, beta_in, final, totals,
+           cost, gamma, beta, cost_b, tabs, kept, recv, send, work, qbuf, angle, lane_mix, lane_sum, acc, part, gath,
+           load_sem, send_sem, recv_sem, cost_send, cost_recv, sum_send, sum_recv):
     nb = ny * nx
     chips = nx // 2
     last = num_layers - 1
@@ -85,6 +85,10 @@
     dx_order = sorted(range(chips), key=lambda d: -min(d, chips - d))
     offsets = [(dy, dx, dc) for dy in dy_order for dx in dx_order for dc in (1, 0) if dy or dx or dc]
 
+    inputs = [pltpu.make_async_copy(src, dst, load_sem.at[n])
+              for n, (src, dst) in enumerate([(gamma_in, gamma), (beta_in, beta), (cost_in, cost)])]
+    for copy in inputs:
+        copy.start()
     barrier = pltpu.get_barrier_semaphore()
     for dy, dx, dc in offsets:
         y, x, _ = peer(dy, dx, dc)
@@ -172,19 +176,36 @@
         for c in range(2):
             ref[h, pl.ds(y * nx, nx), c] = row[c]
 
-    def send_half(par, h, tan_half):
-        for dy in dy_order:
+    waves = [dy_order[:1]] + [dy_order[i:i + 2] for i in range(1, ny, 2)]
+
+    def mix_lanes(rows, layer):
+        x = jnp.concatenate([jnp.concatenate([re.reshape(nx * 8, LANES), im.reshape(nx * 8, LANES)], axis=1)
+                             for re, im in rows], axis=0)
+        x = matmul(x, lane_mix[layer])
+        parts = [x[n * nx * 8:(n + 1) * nx * 8] for n in range(len(rows))]
+        return [(p[:, :LANES].reshape(nx, 8, LANES), p[:, LANES:].reshape(nx, 8, LANES)) for p in parts]
+
+    def send_half(par, h, layer, tan_half):
+        rows = {dy: mix_leading(*load_row(work, h, (my_y + dy) % ny), tan_half, nx) for dy in dy_order}
+
+        def leave(wave, dy):
             y = (my_y + dy) % ny
-            re, im = load_row(work, h, y)
-            store_row(send.at[par], h, y, mix_leading(re, im, tan_half, nx))
+            store_row(send.at[par], h, y, rows[dy])
             for dx in dx_order:
                 for dc in (1, 0):
                     if dy or dx or dc:
                         _, x, dest = peer(dy, dx, dc)
                         pltpu.make_async_remote_copy(
                             src_ref=send.at[par, h, dest], dst_ref=recv.at[par, h, me],
-                            send_sem=send_sem.at[par, h], recv_sem=recv_sem.at[par, h, me],
+                            send_sem=send_sem.at[par, h], recv_sem=recv_sem.at[par, h, wave],
                             device_id={"qy": y, "qx": x}, device_id_type=MESH_ID).start()
+
+        leave(0, dy_order[0])
+        rest = dy_order[1:]
+        rows.update(zip(rest, mix_lanes([rows[dy] for dy in rest], layer)))
+        for n, wave in enumerate(waves[1:]):
+            for dy in wave:
+                leave(n + 1, dy)
         for c in range(2):
             recv[par, h, me, c] = send[par, h, me, c]
 
@@ -193,36 +214,29 @@
         pltpu.make_async_copy(view, view, send_sem.at[par, h]).wait()
 
     sub = lax.broadcasted_iota(jnp.int32, (nx, 8, LANES), 1)
-    source_order = [(ny - dy) % ny for dy in dy_order]
-    waves = [source_order[i:i + 2] for i in range(0, ny, 2)]
 
     def receive(par, h, layer, tan_half):
-        for wave in waves:
-            rows = []
+        for n, wave in enumerate(waves):
+            count = len(wave) * nx - (1 if 0 in wave else 0)
+            view = recv.at[par, h, pl.ds(0, count)]
+            pltpu.make_async_copy(view, view, recv_sem.at[par, h, n]).wait()
             for dy in wave:
-                y = (my_y + dy) % ny
-                for dx in dx_order:
-                    for dc in (1, 0):
-                        if dy or dx or dc:
-                            slot = peer(dy, dx, dc)[2]
-                            view = recv.at[par, h, slot]
-                            pltpu.make_async_copy(view, view, recv_sem.at[par, h, slot]).wait()
+                y = (my_y + ny - dy) % ny
                 re, im = load_row(recv.at[par], h, y)
                 for dist in (1, 2, 4):
                     re, im = (re + tan_half * sublane_partner(im, sub, dist),
                               im - tan_half * sublane_partner(re, sub, dist))
                 re, im = mix_leading(re, im, tan_half, nx)
-                rows.append(jnp.concatenate([re.reshape(nx * 8, LANES), im.reshape(nx * 8, LANES)], axis=1))
-            mixed = matmul(jnp.concatenate(rows, axis=0), lane_mix[layer])
-            for k, dy in enumerate(wave):
-                part_rows = mixed[k * nx * 8:(k + 1) * nx * 8]
-                store_row(work, h, (my_y + dy) % ny, (part_rows[:, :LANES].reshape(nx, 8, LANES),
-                                                      part_rows[:, LANES:].reshape(nx, 8, LANES)))
+                if n == 0:
+                    re, im = mix_lanes([(re, im)], layer)[0]
+                store_row(work, h, y, (re, im))
 
     def per_half(body):
         lax.fori_loop(0, 2, lambda h, _: (body(h), 0)[1], 0)
 
-    make_angle(0)
+    for copy in inputs:
+        copy.wait()
+    make_lanes()
     make_table(0, cost)
     tan0 = angle[0, 0]
 
@@ -241,15 +255,13 @@
     for dy, dx, dc in offsets:
         y, x, dest = peer(dy, dx, dc)
         pltpu.make_async_remote_copy(
-            src_ref=cost.at[dest], dst_ref=cost_b.at[me], send_sem=cost_send, recv_sem=cost_recv.at[me],
+            src_ref=cost.at[dest], dst_ref=cost_b.at[me], send_sem=cost_send, recv_sem=cost_recv,
             device_id={"qy": y, "qx": x}, device_id_type=MESH_ID).start()
     for h in range(2):
         cost_b[me, h] = cost[me, h]
-    per_half(lambda h: send_half(0, h, tan0))
-    make_lanes()
-    for dy, dx, dc in offsets:
-        slot = peer(dy, dx, dc)[2]
-        pltpu.make_async_copy(cost_b.at[slot], cost_b.at[slot], cost_recv.at[slot]).wait()
+    per_half(lambda h: send_half(0, h, 0, tan0))
+    view = cost_b.at[pl.ds(0, nb - 1)]
+    pltpu.make_async_copy(view, view, cost_recv).wait()
     make_table(1, cost_b)
 
     before_at, lam_pre, lam = num_layers, 2 * num_layers, 2 * num_layers + 1
@@ -285,8 +297,6 @@
         energy = acc[0]
         for (h, j), (re, im) in zip(places, blocks):
             c = cost[j, h]
-            final[0, j, h] = root * re
-            final[1, j, h] = root * im
             conj.append((c * re, -(c * im)))
             energy += c * (re * re + im * im)
         acc[0] = energy
@@ -386,7 +396,7 @@
             def _():
                 wait_sends(1, h)
 
-            send_half(1, h, tan_next)
+            send_half(1, h, following, tan_next)
 
         per_half(half)
 
@@ -414,17 +424,28 @@
 
         @pl.when(k < 2 * pairs - 1)
         def _():
-            tan_next = angle[following - (k // (pairs - 1)) * (1 - k // pairs) * (following - last), 0]
+            into = following - (k // (pairs - 1)) * (1 - k // pairs) * (following - last)
+            tan_next = angle[into, 0]
 
             def half_joint(h):
                 wait_sends(0, h)
-                send_half(0, h, tan_next)
+                send_half(0, h, into, tan_next)
 
             per_half(half_joint)
 
         @pl.when(k < pairs - 1)
         def _():
             make_table(step + 2, cost_b)
+
+        @pl.when(k == pairs - 1)
+        def _():
+            def write(j, _):
+                for h in range(2):
+                    for c in range(2):
+                        final[c, j, h] = root * kept[last, h, j, c]
+                return 0
+
+            lax.fori_loop(0, nb, write, 0)
 
         @pl.when((k >= pairs) & (k < 2 * pairs - 1))
         def _():
@@ -450,7 +471,7 @@
     for dy, dx, dc in offsets:
         y, x, dest = peer(dy, dx, dc)
         pltpu.make_async_remote_copy(
-            src_ref=part, dst_ref=gath.at[me], send_sem=sum_send, recv_sem=sum_recv.at[me],
+            src_ref=part, dst_ref=gath.at[me], send_sem=sum_send, recv_sem=sum_recv,
             device_id={"qy": y, "qx": x}, device_id_type=MESH_ID).start()
     gath[me] = row
     for par in range(2):
@@ -458,9 +479,8 @@
             wait_sends(par, h)
     view = cost_b.at[pl.ds(0, nb - 1)]
     pltpu.make_async_copy(view, view, cost_send).wait()
-    for dy, dx, dc in offsets:
-        slot = peer(dy, dx, dc)[2]
-        pltpu.make_async_copy(part, gath.at[slot], sum_recv.at[slot]).wait()
+    view = gath.at[pl.ds(0, nb - 1)]
+    pltpu.make_async_copy(view, view, sum_recv).wait()
     total = gath[0]
     for j in range(1, nb):
         total += gath[j]
@@ -485,9 +505,12 @@
         final, totals = pl.pallas_call(
             functools.partial(kernel, ny, nx, num_layers, num_qubits, amp),
             out_shape=(jax.ShapeDtypeStruct((2, nb, 2, 8, LANES), f32), jax.ShapeDtypeStruct((1, LANES), f32)),
-            in_specs=[pl.BlockSpec(memory_space=vmem), pl.BlockSpec(memory_space=smem), pl.BlockSpec(memory_space=smem)],
+            in_specs=[pl.BlockSpec(memory_space=pl.ANY)] * 3,
             out_specs=(pl.BlockSpec(memory_space=vmem), pl.BlockSpec(memory_space=vmem)),
             scratch_shapes=[
+                vmem((nb, 2, 8, LANES), f32),
+                smem((num_layers,), f32),
+                smem((num_layers,), f32),
                 vmem((nb, 2, 8, LANES), f32),
                 vmem((num_layers, 2, 2, nb, 8, LANES), f32),
                 vmem((2 * num_layers + 2,) + state, f32),
@@ -501,12 +524,13 @@
                 vmem((1 + 2 * num_layers, 8, LANES), f32),
                 vmem((1, LANES), f32),
                 vmem((nb, 1, LANES), f32),
+                dma((3,)),
                 dma((2, 2)),
-                dma((2, 2, nb)),
+                dma((2, 2, 1 + ny // 2)),
                 dma,
-                dma((nb,)),
                 dma,
-                dma((nb,)),
+                dma,
+                dma,
             ],
             compiler_params=pltpu.CompilerParams(
                 collective_id=0, has_side_effects=True, vmem_limit_bytes=48 * 1024 * 1024),

time: 165 us -> 154 us (0.933)
  Pallas kernels: 160 us -> 149 us
    pallas_call x1, Pallas kernels: 160 us -> 149 us  [local_run(): pl.pallas_call(functools.partial(kernel, ny, nx, num_layers, num_qubits,...]
where the time goes in v4:
time: 154 us
  Pallas kernels  149 us (97%)
  local copies, waits for them, and re-layouts  3.38 us (2%)
  between operations  1.82 us (1%)
    pallas_call x1, Pallas kernels, local_run(): pl.pallas_call(functools.partial(kernel, ny, nx, num_layers, num_qubits,...  149 us

profile of v4, /device:TPU:97, one launch (start us, length us, event | category | flops | bytes accessed | tf_op | source)
XLA Modules:
  0.0 154.0 jit_solution(10255023756108667601)
XLA Ops:
  0.6 0.0 copy-start.2
  0.6 0.0 copy-start.1
  0.6 0.6 copy-done.2
  1.3 0.0 copy-done.1
  1.3 0.0 copy-start
  1.3 0.9 copy-done
  2.3 148.8 %qaoa.1 = (f32[2,32,2,8,128]{4,3,2,1,0:T(8,128)S(1)}, f32[1,128]{1,0:T(1,128)S(1)}) custom-call(f32[32,2,8,128]{3,2,1,0:T(8,128)S(1)} %bitcast.11, f32[8]{0:T(128)S(1)} %copy-done.1, f32[8]{0:T(128)S(1)} %copy-done.2), custom_call_target="tpu_custom_call" | custom-call | tf_op jit(solution)/shard_map/qaoa/pallas_call | solution.py:505
  151.0 1.2 copy.8
  152.2 0.6 slice_bitcast_fusion
Async XLA Ops:
  0.6 0.7 copy-start.2
  0.6 0.7 copy-start.1
  1.3 0.9 copy-start

commit v5 on v4

--- a/solution.py
+++ b/solution.py
@@ -66,7 +66,7 @@
 
 
 def kernel(ny, nx, num_layers, num_qubits, amp, cost_in, gamma_in, beta_in, final, totals,
-           cost, gamma, beta, cost_b, tabs, kept, recv, send, work, qbuf, angle, lane_mix, lane_sum, acc, part, gath,
+           cost, gamma, beta, cost_b, tabs, kept, recv, send, work, side, qbuf, angle, lane_mix, lane_sum, acc, part, gath,
            load_sem, send_sem, recv_sem, cost_send, cost_recv, sum_send, sum_recv):
     nb = ny * nx
     chips = nx // 2
@@ -185,8 +185,8 @@
         parts = [x[n * nx * 8:(n + 1) * nx * 8] for n in range(len(rows))]
         return [(p[:, :LANES].reshape(nx, 8, LANES), p[:, LANES:].reshape(nx, 8, LANES)) for p in parts]
 
-    def send_half(par, h, layer, tan_half):
-        rows = {dy: mix_leading(*load_row(work, h, (my_y + dy) % ny), tan_half, nx) for dy in dy_order}
+    def send_half(par, h, layer, tan_half, source):
+        rows = {dy: mix_leading(*load_row(source, h, (my_y + dy) % ny), tan_half, nx) for dy in dy_order}
 
         def leave(wave, dy):
             y = (my_y + dy) % ny
@@ -215,7 +215,7 @@
 
     sub = lax.broadcasted_iota(jnp.int32, (nx, 8, LANES), 1)
 
-    def receive(par, h, layer, tan_half):
+    def receive(par, h, layer, tan_half, target):
         for n, wave in enumerate(waves):
             count = len(wave) * nx - (1 if 0 in wave else 0)
             view = recv.at[par, h, pl.ds(0, count)]
@@ -229,7 +229,7 @@
                 re, im = mix_leading(re, im, tan_half, nx)
                 if n == 0:
                     re, im = mix_lanes([(re, im)], layer)[0]
-                store_row(work, h, y, (re, im))
+                store_row(target, h, y, (re, im))
 
     def per_half(body):
         lax.fori_loop(0, 2, lambda h, _: (body(h), 0)[1], 0)
@@ -259,12 +259,13 @@
             device_id={"qy": y, "qx": x}, device_id_type=MESH_ID).start()
     for h in range(2):
         cost_b[me, h] = cost[me, h]
-    per_half(lambda h: send_half(0, h, 0, tan0))
+    per_half(lambda h: send_half(0, h, 0, tan0, work))
     view = cost_b.at[pl.ds(0, nb - 1)]
     pltpu.make_async_copy(view, view, cost_recv).wait()
     make_table(1, cost_b)
 
-    before_at, lam_pre, lam = num_layers, 2 * num_layers, 2 * num_layers + 1
+    before_at, lam_pre, lam, side_at, sums_at = (num_layers, 2 * num_layers, 2 * num_layers + 1,
+                                                 2 * num_layers + 2, 2 * num_layers + 4)
     root = jnp.float32(1.0 / amp)
     zero = jnp.zeros((8, LANES), jnp.float32)
     pairs = num_layers // 2
@@ -322,24 +323,16 @@
 
         lax.fori_loop(0, nx, body, 0)
 
-    def prepare(layer):
+    def low_sums(at):
         def low(n, _):
             h, y = n // ny, n % ny
-            re, im = load_row(kept.at[layer], h, y)
+            re, im = load_row(kept.at[at], h, y)
             store_row(qbuf, h, y, sums_of(re, im, nx))
             return 0
 
         lax.fori_loop(0, 2 * ny, low, 0)
-        high_sums(layer)
-
-        def body(j, total):
-            for h in range(2):
-                total += im_dot((kept[lam, h, j, 0], kept[lam, h, j, 1]), (qbuf[h, j, 0], qbuf[h, j, 1]))
-            return total
-
-        acc[1 + num_layers + layer] = lax.fori_loop(0, nb, body, zero)
-        at = before_at + layer
-
+
+    def full_sums(at):
         def inner(y, _):
             rows = [load_row(kept.at[at], h, y) for h in range(2)]
             x = jnp.concatenate([jnp.concatenate([re.reshape(nx * 8, LANES), im.reshape(nx * 8, LANES)], axis=1)
@@ -359,6 +352,18 @@
         lax.fori_loop(0, ny, inner, 0)
         high_sums(at)
 
+    def prepare(layer):
+        low_sums(layer)
+        high_sums(layer)
+
+        def body(j, total):
+            for h in range(2):
+                total += im_dot((kept[lam, h, j, 0], kept[lam, h, j, 1]), (qbuf[h, j, 0], qbuf[h, j, 1]))
+            return total
+
+        acc[1 + num_layers + layer] = lax.fori_loop(0, nb, body, zero)
+        full_sums(before_at + layer)
+
     def collect(layer, source):
         at = before_at + layer
 
@@ -374,14 +379,62 @@
         acc[1 + layer] = 2.0 * gamma_sum
         acc[1 + num_layers + layer] += beta_sum
 
-    def last_sums(x, sums):
-        gamma_sum, beta_sum = sums
-        places = column(x, (0, 1))
-        blocks = scaled(mix_all(load(work, places), angle[0, 0]), angle[0, 1])
-        for (h, j), left, right, q in zip(places, blocks, load(kept.at[before_at], places), load(qbuf, places)):
-            gamma_sum += cost[j, h] * im_dot(left, right)
-            beta_sum += im_dot(left, q)
-        return gamma_sum, beta_sum
+    def side_source(k):
+        @pl.when(k == 0)
+        def _():
+            def body(places):
+                blocks = [(cost[j, h] * re, cost[j, h] * im)
+                          for (h, j), (re, im) in zip(places, load(kept.at[before_at], places))]
+                store(side, places, mix_all(blocks, tan0))
+
+            for_columns((0, 1), body)
+
+        @pl.when(k == 2)
+        def _():
+            low_sums(before_at)
+            high_sums(before_at)
+            for_columns((0, 1), lambda places: store(side, places, mix_all(load(qbuf, places), tan0)))
+
+    def side_arrival(n):
+        per_half(lambda h: receive(2 + n, h, 0, tan0, side))
+
+        def body(places):
+            for h in range(2):
+                mine = places[h::2]
+                store(kept.at[side_at + n], mine, scaled(mix_all(load(side, mine), tan0), angle[0, 1]))
+
+        for_columns((0, 1), body)
+
+    def side_sums():
+        full_sums(0)
+
+        def body(j, _):
+            for h in range(2):
+                for c in range(2):
+                    kept[sums_at, h, j, c] = qbuf[h, j, c] + kept[side_at + 1, h, j, c]
+            return 0
+
+        lax.fori_loop(0, nb, body, 0)
+
+    def last_sums(h):
+        def body(x, sums):
+            gamma1, beta1, gamma0, beta0 = sums
+            places = column(x, (h,))
+            blocks = scaled(mix_all(load(work, places), angle[1, 0]), angle[1, 1])
+            for (h_, j), left, right, q in zip(places, blocks, load(kept.at[before_at + 1], places), load(qbuf, places)):
+                gamma1 += cost_b[j, h_] * im_dot(left, right)
+                beta1 += im_dot(left, q)
+            blocks = turn(blocks, 1, places)
+            for left, right, q in zip(blocks, load(kept.at[side_at], places), load(kept.at[sums_at], places)):
+                gamma0 += im_dot(left, right)
+                beta0 += im_dot(left, q)
+            return gamma1, beta1, gamma0, beta0
+
+        gamma1, beta1, gamma0, beta0 = lax.fori_loop(0, nx, body, (zero,) * 4)
+        acc[1] += 2.0 * gamma0
+        acc[2] += 2.0 * gamma1
+        acc[1 + num_layers] += beta0
+        acc[2 + num_layers] += beta1
 
     def two_gaps(k, _):
         step = 2 * k
@@ -389,16 +442,22 @@
         tan_half, tan_next = angle[done, 0], angle[following, 0]
 
         def half(h):
-            receive(0, h, done, tan_half)
+            receive(0, h, done, tan_half, work)
             for_columns((h,), middle(step))
 
             @pl.when(k > 0)
             def _():
                 wait_sends(1, h)
 
-            send_half(1, h, following, tan_next)
+            send_half(1, h, following, tan_next, work)
 
         per_half(half)
+
+        side_source(k)
+
+        @pl.when(k < 4)
+        def _():
+            send_half(2 + k // 2, k % 2, 0, tan0, side)
 
         @pl.when(k < pairs - 1)
         def _():
@@ -412,7 +471,7 @@
         step = 2 * k + 1
         _, done, _, following = plan(step)
         tan_half = angle[done, 0]
-        per_half(lambda h: receive(1, h, done, tan_half))
+        per_half(lambda h: receive(1, h, done, tan_half, work))
 
         @pl.when(k % pairs < pairs - 1)
         def _():
@@ -422,16 +481,14 @@
         def _():
             for_columns((0, 1), turn_point)
 
-        @pl.when(k < 2 * pairs - 1)
-        def _():
-            into = following - (k // (pairs - 1)) * (1 - k // pairs) * (following - last)
-            tan_next = angle[into, 0]
-
-            def half_joint(h):
-                wait_sends(0, h)
-                send_half(0, h, into, tan_next)
-
-            per_half(half_joint)
+        into = following - (k // (pairs - 1)) * (1 - k // pairs) * (following - last)
+        tan_next = angle[into, 0]
+
+        def half_joint(h):
+            wait_sends(0, h)
+            send_half(0, h, into, tan_next, work)
+
+        per_half(half_joint)
 
         @pl.when(k < pairs - 1)
         def _():
@@ -447,20 +504,31 @@
 
             lax.fori_loop(0, nb, write, 0)
 
-        @pl.when((k >= pairs) & (k < 2 * pairs - 1))
+        @pl.when(k >= pairs)
         def _():
             collect(done, cost)
 
-        @pl.when((k >= pairs - 1) & (k < 2 * pairs - 1))
+        @pl.when((k == 4) | (k == 5))
+        def _():
+            side_arrival(k - 4)
+
+        @pl.when(k == 2 * pairs - 2)
+        def _():
+            side_sums()
+
+        @pl.when(k >= pairs - 1)
         def _():
             prepare(2 * num_layers - 3 - 2 * k)
 
         return 0
 
-    lax.fori_loop(0, 2 * pairs, two_gaps, 0)
-    gamma_sum, beta_sum = lax.fori_loop(0, nx, last_sums, (zero, zero))
-    acc[1] = 2.0 * gamma_sum
-    acc[1 + num_layers] += beta_sum
+    lax.fori_loop(0, 2 * pairs - 1, two_gaps, 0)
+
+    def last_half(h):
+        receive(0, h, 1, angle[1, 0], work)
+        last_sums(h)
+
+    per_half(last_half)
 
     lane = lax.broadcasted_iota(jnp.int32, (1, LANES), 1)
     row = jnp.zeros((1, LANES), jnp.float32)
@@ -474,7 +542,7 @@
             src_ref=part, dst_ref=gath.at[me], send_sem=sum_send, recv_sem=sum_recv,
             device_id={"qy": y, "qx": x}, device_id_type=MESH_ID).start()
     gath[me] = row
-    for par in range(2):
+    for par in range(4):
         for h in range(2):
             wait_sends(par, h)
     view = cost_b.at[pl.ds(0, nb - 1)]
@@ -496,7 +564,7 @@
     def local_run(cost_local, gamma_angles, beta_angles):
         chunk = cost_local.shape[0]
         num_layers = gamma_angles.shape[0]
-        assert chunk == nb * 16 * LANES and num_layers % 2 == 0
+        assert chunk == nb * 16 * LANES and num_layers % 2 == 0 and num_layers >= 8
         num_qubits = int(math.log2(chunk * nb))
         amp = (chunk * nb) ** -0.5
         vmem, smem, dma = pltpu.VMEM, pltpu.SMEM, pltpu.SemaphoreType.DMA
@@ -505,7 +573,7 @@
         final, totals = pl.pallas_call(
             functools.partial(kernel, ny, nx, num_layers, num_qubits, amp),
             out_shape=(jax.ShapeDtypeStruct((2, nb, 2, 8, LANES), f32), jax.ShapeDtypeStruct((1, LANES), f32)),
-            in_specs=[pl.BlockSpec(memory_space=pl.ANY)] * 3,
+            in_specs=[pl.BlockSpec(memory_space=pltpu.MemorySpace.HBM)] * 3,
             out_specs=(pl.BlockSpec(memory_space=vmem), pl.BlockSpec(memory_space=vmem)),
             scratch_shapes=[
                 vmem((nb, 2, 8, LANES), f32),
@@ -513,9 +581,10 @@
                 smem((num_layers,), f32),
                 vmem((nb, 2, 8, LANES), f32),
                 vmem((num_layers, 2, 2, nb, 8, LANES), f32),
-                vmem((2 * num_layers + 2,) + state, f32),
-                vmem((2,) + state, f32),
-                vmem((2,) + state, f32),
+                vmem((2 * num_layers + 5,) + state, f32),
+                vmem((4,) + state, f32),
+                vmem((4,) + state, f32),
+                vmem(state, f32),
                 vmem(state, f32),
                 vmem(state, f32),
                 vmem((num_layers, 2, 8, LANES), f32),
@@ -525,8 +594,8 @@
                 vmem((1, LANES), f32),
                 vmem((nb, 1, LANES), f32),
                 dma((3,)),
-                dma((2, 2)),
-                dma((2, 2, 1 + ny // 2)),
+                dma((4, 2)),
+                dma((4, 2, 1 + ny // 2)),
                 dma,
                 dma,
                 dma,

time: 154 us -> 152 us (0.987)
  Pallas kernels: 149 us -> 147 us
    pallas_call x1, Pallas kernels: 149 us -> 147 us  [local_run(): pl.pallas_call(functools.partial(kernel, ny, nx, num_layers, num_qubits,...]
where the time goes in v5:
time: 152 us
  Pallas kernels  147 us (97%)
  local copies, waits for them, and re-layouts  3.38 us (2%)
  between operations  1.82 us (1%)
    pallas_call x1, Pallas kernels, local_run(): pl.pallas_call(functools.partial(kernel, ny, nx, num_layers, num_qubits,...  147 us

profile of v5, /device:TPU:97, one launch (start us, length us, event | category | flops | bytes accessed | tf_op | source)
XLA Modules:
  0.0 152.2 jit_solution(13496427584831280534)
XLA Ops:
  0.6 0.0 copy-start.2
  0.6 0.0 copy-start.1
  0.6 0.6 copy-done.2
  1.3 0.0 copy-done.1
  1.3 0.0 copy-start
  1.3 0.9 copy-done
  2.3 147.0 %qaoa.1 = (f32[2,32,2,8,128]{4,3,2,1,0:T(8,128)S(1)}, f32[1,128]{1,0:T(1,128)S(1)}) custom-call(f32[32,2,8,128]{3,2,1,0:T(8,128)S(1)} %bitcast.11, f32[8]{0:T(128)S(1)} %copy-done.1, f32[8]{0:T(128)S(1)} %copy-done.2), custom_call_target="tpu_custom_call" | custom-call | tf_op jit(solution)/shard_map/qaoa/pallas_call | solution.py:573
  149.2 1.2 copy.8
  150.4 0.6 slice_bitcast_fusion
Async XLA Ops:
  0.6 0.7 copy-start.2
  0.6 0.7 copy-start.1
  1.3 0.9 copy-start

commit v6 on v5

--- a/solution.py
+++ b/solution.py
@@ -106,15 +106,10 @@
         angle[layer, 1] = scale
         return cos_half[:1], sin_half[:1]
 
-    def make_lanes():
+    def make_lanes(layers):
         flips = lax.broadcasted_iota(jnp.int32, (LANES, LANES), 0) ^ lax.broadcasted_iota(jnp.int32, (LANES, LANES), 1)
         weight = sum((flips >> bit) & 1 for bit in range(7))
-        ones = jnp.where(weight == 1, 1.0, 0.0).astype(jnp.float32)
-        lane_sum[:LANES, :LANES] = ones
-        lane_sum[LANES:, LANES:] = ones
-        lane_sum[:LANES, LANES:] = jnp.zeros_like(ones)
-        lane_sum[LANES:, :LANES] = jnp.zeros_like(ones)
-        for layer in range(num_layers):
+        for layer in layers:
             c, s = make_angle(layer)
             coefs = []
             for k in range(8):
@@ -132,6 +127,12 @@
             lane_mix[layer, LANES:, LANES:] = even
             lane_mix[layer, LANES:, :LANES] = odd
             lane_mix[layer, :LANES, LANES:] = -odd
+        if 0 not in layers:
+            ones = jnp.where(weight == 1, 1.0, 0.0).astype(jnp.float32)
+            lane_sum[:LANES, :LANES] = ones
+            lane_sum[LANES:, LANES:] = ones
+            lane_sum[:LANES, LANES:] = jnp.zeros_like(ones)
+            lane_sum[LANES:, :LANES] = jnp.zeros_like(ones)
 
     def make_table(layer, source):
         g = gamma[layer]
@@ -167,7 +168,7 @@
         return [(h, y * nx + x) for y in range(ny) for h in halves]
 
     def for_columns(halves, body):
-        lax.fori_loop(0, nx, lambda x, _: (body(column(x, halves)), 0)[1], 0)
+        lax.fori_loop(0, nx, lambda x, _: (body(column(x, halves)), 0)[1], 0, unroll=2)
 
     def load_row(ref, h, y):
         return ref[h, pl.ds(y * nx, nx), 0], ref[h, pl.ds(y * nx, nx), 1]
@@ -236,7 +237,7 @@
 
     for copy in inputs:
         copy.wait()
-    make_lanes()
+    make_lanes([0])
     make_table(0, cost)
     tan0 = angle[0, 0]
 
@@ -260,6 +261,7 @@
     for h in range(2):
         cost_b[me, h] = cost[me, h]
     per_half(lambda h: send_half(0, h, 0, tan0, work))
+    make_lanes(range(1, num_layers))
     view = cost_b.at[pl.ds(0, nb - 1)]
     pltpu.make_async_copy(view, view, cost_recv).wait()
     make_table(1, cost_b)
@@ -455,10 +457,6 @@
 
         side_source(k)
 
-        @pl.when(k < 4)
-        def _():
-            send_half(2 + k // 2, k % 2, 0, tan0, side)
-
         @pl.when(k < pairs - 1)
         def _():
             make_table(step + 2, cost)
@@ -467,6 +465,11 @@
         def _():
             collect(done, cost_b)
             prepare(following)
+
+        @pl.when((k < 3) | (k == 4))
+        def _():
+            piece = k - k // 4
+            send_half(2 + piece // 2, piece % 2, 0, tan0, side)
 
         step = 2 * k + 1
         _, done, _, following = plan(step)

time: 152 us -> 152 us (level)
  no operation moved by 1% of the time
where the time goes in v6:
time: 152 us; the launch traced here: 151 us
  Pallas kernels  146 us (96%)
  local copies, waits for them, and re-layouts  3.38 us (2%)
  between operations  1.82 us (1%)
    pallas_call x1, Pallas kernels, local_run(): pl.pallas_call(functools.partial(kernel, ny, nx, num_layers, num_qubits,...  146 us

profile of v6, /device:TPU:97, one launch (start us, length us, event | category | flops | bytes accessed | tf_op | source)
XLA Modules:
  0.0 151.4 jit_solution(9283646285857027885)
XLA Ops:
  0.6 0.0 copy-start.2
  0.6 0.0 copy-start.1
  0.6 0.6 copy-done.2
  1.3 0.0 copy-done.1
  1.3 0.0 copy-start
  1.3 0.9 copy-done
  2.3 146.2 %qaoa.1 = (f32[2,32,2,8,128]{4,3,2,1,0:T(8,128)S(1)}, f32[1,128]{1,0:T(1,128)S(1)}) custom-call(f32[32,2,8,128]{3,2,1,0:T(8,128)S(1)} %bitcast.11, f32[8]{0:T(128)S(1)} %copy-done.1, f32[8]{0:T(128)S(1)} %copy-done.2), custom_call_target="tpu_custom_call" | custom-call | tf_op jit(solution)/shard_map/qaoa/pallas_call | solution.py:576
  148.5 1.2 copy.8
  149.7 0.6 slice_bitcast_fusion
Async XLA Ops:
  0.6 0.7 copy-start.2
  0.6 0.7 copy-start.1
  1.3 0.9 copy-start

commit v7 on v6

--- a/solution.py
+++ b/solution.py
@@ -186,7 +186,10 @@
         parts = [x[n * nx * 8:(n + 1) * nx * 8] for n in range(len(rows))]
         return [(p[:, :LANES].reshape(nx, 8, LANES), p[:, LANES:].reshape(nx, 8, LANES)) for p in parts]
 
-    def send_half(par, h, layer, tan_half, source):
+    def lanes_late(even, h):
+        return [] if h else waves[:1] if even else waves
+
+    def send_half(par, h, layer, tan_half, source, late):
         rows = {dy: mix_leading(*load_row(source, h, (my_y + dy) % ny), tan_half, nx) for dy in dy_order}
 
         def leave(wave, dy):
@@ -201,12 +204,13 @@
                             send_sem=send_sem.at[par, h], recv_sem=recv_sem.at[par, h, wave],
                             device_id={"qy": y, "qx": x}, device_id_type=MESH_ID).start()
 
-        leave(0, dy_order[0])
-        rest = dy_order[1:]
-        rows.update(zip(rest, mix_lanes([rows[dy] for dy in rest], layer)))
-        for n, wave in enumerate(waves[1:]):
-            for dy in wave:
-                leave(n + 1, dy)
+        for group in (waves[:1], waves[1:]):
+            early = [dy for wave in group if wave not in late for dy in wave]
+            if early:
+                rows.update(zip(early, mix_lanes([rows[dy] for dy in early], layer)))
+            for wave in group:
+                for dy in wave:
+                    leave(waves.index(wave), dy)
         for c in range(2):
             recv[par, h, me, c] = send[par, h, me, c]
 
@@ -216,7 +220,8 @@
 
     sub = lax.broadcasted_iota(jnp.int32, (nx, 8, LANES), 1)
 
-    def receive(par, h, layer, tan_half, target):
+    def receive(par, h, layer, tan_half, target, late):
+        late_rows = []
         for n, wave in enumerate(waves):
             count = len(wave) * nx - (1 if 0 in wave else 0)
             view = recv.at[par, h, pl.ds(0, count)]
@@ -228,9 +233,13 @@
                     re, im = (re + tan_half * sublane_partner(im, sub, dist),
                               im - tan_half * sublane_partner(re, sub, dist))
                 re, im = mix_leading(re, im, tan_half, nx)
-                if n == 0:
-                    re, im = mix_lanes([(re, im)], layer)[0]
-                store_row(target, h, y, (re, im))
+                if wave in late:
+                    late_rows.append((y, (re, im)))
+                else:
+                    store_row(target, h, y, (re, im))
+        if late_rows:
+            for (y, _), row in zip(late_rows, mix_lanes([row for _, row in late_rows], layer)):
+                store_row(target, h, y, row)
 
     def per_half(body):
         lax.fori_loop(0, 2, lambda h, _: (body(h), 0)[1], 0)
@@ -260,7 +269,8 @@
             device_id={"qy": y, "qx": x}, device_id_type=MESH_ID).start()
     for h in range(2):
         cost_b[me, h] = cost[me, h]
-    per_half(lambda h: send_half(0, h, 0, tan0, work))
+    for h in range(2):
+        send_half(0, h, 0, tan0, work, lanes_late(True, h))
     make_lanes(range(1, num_layers))
     view = cost_b.at[pl.ds(0, nb - 1)]
     pltpu.make_async_copy(view, view, cost_recv).wait()
@@ -398,7 +408,7 @@
             for_columns((0, 1), lambda places: store(side, places, mix_all(load(qbuf, places), tan0)))
 
     def side_arrival(n):
-        per_half(lambda h: receive(2 + n, h, 0, tan0, side))
+        per_half(lambda h: receive(2 + n, h, 0, tan0, side, []))
 
         def body(places):
             for h in range(2):
@@ -444,16 +454,17 @@
         tan_half, tan_next = angle[done, 0], angle[following, 0]
 
         def half(h):
-            receive(0, h, done, tan_half, work)
+            receive(0, h, done, tan_half, work, lanes_late(True, h))
             for_columns((h,), middle(step))
 
             @pl.when(k > 0)
             def _():
                 wait_sends(1, h)
 
-            send_half(1, h, following, tan_next, work)
-
-        per_half(half)
+            send_half(1, h, following, tan_next, work, lanes_late(False, h))
+
+        for h in range(2):
+            half(h)
 
         side_source(k)
 
@@ -469,12 +480,13 @@
         @pl.when((k < 3) | (k == 4))
         def _():
             piece = k - k // 4
-            send_half(2 + piece // 2, piece % 2, 0, tan0, side)
+            send_half(2 + piece // 2, piece % 2, 0, tan0, side, [])
 
         step = 2 * k + 1
         _, done, _, following = plan(step)
         tan_half = angle[done, 0]
-        per_half(lambda h: receive(1, h, done, tan_half, work))
+        for h in range(2):
+            receive(1, h, done, tan_half, work, lanes_late(False, h))
 
         @pl.when(k % pairs < pairs - 1)
         def _():
@@ -489,9 +501,10 @@
 
         def half_joint(h):
             wait_sends(0, h)
-            send_half(0, h, into, tan_next, work)
-
-        per_half(half_joint)
+            send_half(0, h, into, tan_next, work, lanes_late(True, h))
+
+        for h in range(2):
+            half_joint(h)
 
         @pl.when(k < pairs - 1)
         def _():
@@ -528,10 +541,11 @@
     lax.fori_loop(0, 2 * pairs - 1, two_gaps, 0)
 
     def last_half(h):
-        receive(0, h, 1, angle[1, 0], work)
+        receive(0, h, 1, angle[1, 0], work, lanes_late(True, h))
         last_sums(h)
 
-    per_half(last_half)
+    for h in range(2):
+        last_half(h)
 
     lane = lax.broadcasted_iota(jnp.int32, (1, LANES), 1)
     row = jnp.zeros((1, LANES), jnp.float32)

time: 152 us -> 151 us (level)
  no operation moved by 1% of the time
where the time goes in v7:
time: 151 us; the launch traced here: 150 us
  Pallas kernels  145 us (96%)
  local copies, waits for them, and re-layouts  3.38 us (2%)
  between operations  1.82 us (1%)
    pallas_call x1, Pallas kernels, local_run(): pl.pallas_call(functools.partial(kernel, ny, nx, num_layers, num_qubits,...  145 us

profile of v7, /device:TPU:97, one launch (start us, length us, event | category | flops | bytes accessed | tf_op | source)
XLA Modules:
  0.0 150.4 jit_solution(3042666849377352894)
XLA Ops:
  0.6 0.0 copy-start.2
  0.6 0.0 copy-start.1
  0.6 0.6 copy-done.2
  1.3 0.0 copy-done.1
  1.3 0.0 copy-start
  1.3 0.9 copy-done
  2.3 145.2 %qaoa.1 = (f32[2,32,2,8,128]{4,3,2,1,0:T(8,128)S(1)}, f32[1,128]{1,0:T(1,128)S(1)}) custom-call(f32[32,2,8,128]{3,2,1,0:T(8,128)S(1)} %bitcast.11, f32[8]{0:T(128)S(1)} %copy-done.1, f32[8]{0:T(128)S(1)} %copy-done.2), custom_call_target="tpu_custom_call" | custom-call | tf_op jit(solution)/shard_map/qaoa/pallas_call | solution.py:590
  147.5 1.2 copy.8
  148.7 0.6 slice_bitcast_fusion
Async XLA Ops:
  0.6 0.7 copy-start.2
  0.6 0.7 copy-start.1
  1.3 0.9 copy-start

commit v8 on v7

--- a/solution.py
+++ b/solution.py
@@ -102,20 +102,19 @@
             if left % 2:
                 scale = power if scale is None else scale * power
             power, left = power * power, left // 2
-        angle[layer, 0] = sin_half / cos_half
-        angle[layer, 1] = scale
-        return cos_half[:1], sin_half[:1]
+        angle[layer] = sin_half / cos_half
+        return cos_half[:1], sin_half[:1], scale[:1]
 
     def make_lanes(layers):
         flips = lax.broadcasted_iota(jnp.int32, (LANES, LANES), 0) ^ lax.broadcasted_iota(jnp.int32, (LANES, LANES), 1)
         weight = sum((flips >> bit) & 1 for bit in range(7))
         for layer in layers:
-            c, s = make_angle(layer)
+            c, s, scale = make_angle(layer)
             coefs = []
             for k in range(8):
-                coef = None
+                coef = scale
                 for factor in [c] * (7 - k) + [s] * k:
-                    coef = factor if coef is None else coef * factor
+                    coef = coef * factor
                 coefs.append(coef if (k // 2) % 2 == 0 else -coef)
             even, odd = jnp.zeros((LANES, LANES), jnp.float32), jnp.zeros((LANES, LANES), jnp.float32)
             for k in range(8):
@@ -161,9 +160,6 @@
             out.append((c * re + s * im, c * im - s * re))
         return out
 
-    def scaled(blocks, scale):
-        return [(scale * re, scale * im) for re, im in blocks]
-
     def column(x, halves):
         return [(h, y * nx + x) for y in range(ny) for h in halves]
 
@@ -190,7 +186,7 @@
         return [] if h else waves[:1] if even else waves
 
     def send_half(par, h, layer, tan_half, source, late):
-        rows = {dy: mix_leading(*load_row(source, h, (my_y + dy) % ny), tan_half, nx) for dy in dy_order}
+        rows = {}
 
         def leave(wave, dy):
             y = (my_y + dy) % ny
@@ -204,7 +200,9 @@
                             send_sem=send_sem.at[par, h], recv_sem=recv_sem.at[par, h, wave],
                             device_id={"qy": y, "qx": x}, device_id_type=MESH_ID).start()
 
-        for group in (waves[:1], waves[1:]):
+        for group in (waves[:1], waves[1:]) if late else (waves,):
+            for dy in [dy for wave in group for dy in wave]:
+                rows[dy] = mix_leading(*load_row(source, h, (my_y + dy) % ny), tan_half, nx)
             early = [dy for wave in group if wave not in late for dy in wave]
             if early:
                 rows.update(zip(early, mix_lanes([rows[dy] for dy in early], layer)))
@@ -237,9 +235,9 @@
                     late_rows.append((y, (re, im)))
                 else:
                     store_row(target, h, y, (re, im))
-        if late_rows:
-            for (y, _), row in zip(late_rows, mix_lanes([row for _, row in late_rows], layer)):
-                store_row(target, h, y, row)
+            if late_rows and wave == late[-1]:
+                for (y, _), row in zip(late_rows, mix_lanes([row for _, row in late_rows], layer)):
+                    store_row(target, h, y, row)
 
     def per_half(body):
         lax.fori_loop(0, 2, lambda h, _: (body(h), 0)[1], 0)
@@ -248,7 +246,7 @@
         copy.wait()
     make_lanes([0])
     make_table(0, cost)
-    tan0 = angle[0, 0]
+    tan0 = angle[0]
 
     def first(places):
         flat = jnp.full((8, LANES), amp, jnp.float32)
@@ -289,12 +287,12 @@
 
     def middle(step):
         back, done, turned, following = plan(step)
-        tan_half, scale, tan_next = angle[done, 0], angle[done, 1], angle[following, 0]
+        tan_half, tan_next = angle[done], angle[following]
         first_at = done + back * (lam_pre - done)
         second_at = before_at + turned + back * (lam - before_at - turned)
 
         def body(places):
-            blocks = scaled(mix_all(load(work, places), tan_half), scale)
+            blocks = mix_all(load(work, places), tan_half)
             store(kept.at[first_at], places, blocks)
             blocks = turn(blocks, turned, places)
             store(kept.at[second_at], places, blocks)
@@ -303,8 +301,8 @@
         return body
 
     def turn_point(places):
-        tan_half, scale = angle[last, 0], angle[last, 1]
-        blocks = scaled(mix_all(load(work, places), tan_half), scale)
+        tan_half = angle[last]
+        blocks = mix_all(load(work, places), tan_half)
         store(kept.at[last], places, blocks)
         conj = []
         energy = acc[0]
@@ -413,7 +411,7 @@
         def body(places):
             for h in range(2):
                 mine = places[h::2]
-                store(kept.at[side_at + n], mine, scaled(mix_all(load(side, mine), tan0), angle[0, 1]))
+                store(kept.at[side_at + n], mine, mix_all(load(side, mine), tan0))
 
         for_columns((0, 1), body)
 
@@ -432,7 +430,7 @@
         def body(x, sums):
             gamma1, beta1, gamma0, beta0 = sums
             places = column(x, (h,))
-            blocks = scaled(mix_all(load(work, places), angle[1, 0]), angle[1, 1])
+            blocks = mix_all(load(work, places), angle[1])
             for (h_, j), left, right, q in zip(places, blocks, load(kept.at[before_at + 1], places), load(qbuf, places)):
                 gamma1 += cost_b[j, h_] * im_dot(left, right)
                 beta1 += im_dot(left, q)
@@ -451,7 +449,7 @@
     def two_gaps(k, _):
         step = 2 * k
         _, done, _, following = plan(step)
-        tan_half, tan_next = angle[done, 0], angle[following, 0]
+        tan_half, tan_next = angle[done], angle[following]
 
         def half(h):
             receive(0, h, done, tan_half, work, lanes_late(True, h))
@@ -484,7 +482,7 @@
 
         step = 2 * k + 1
         _, done, _, following = plan(step)
-        tan_half = angle[done, 0]
+        tan_half = angle[done]
         for h in range(2):
             receive(1, h, done, tan_half, work, lanes_late(False, h))
 
@@ -497,7 +495,7 @@
             for_columns((0, 1), turn_point)
 
         into = following - (k // (pairs - 1)) * (1 - k // pairs) * (following - last)
-        tan_next = angle[into, 0]
+        tan_next = angle[into]
 
         def half_joint(h):
             wait_sends(0, h)
@@ -541,7 +539,7 @@
     lax.fori_loop(0, 2 * pairs - 1, two_gaps, 0)
 
     def last_half(h):
-        receive(0, h, 1, angle[1, 0], work, lanes_late(True, h))
+        receive(0, h, 1, angle[1], work, lanes_late(True, h))
         last_sums(h)
 
     for h in range(2):
@@ -604,7 +602,7 @@
                 vmem(state, f32),
                 vmem(state, f32),
                 vmem(state, f32),
-                vmem((num_layers, 2, 8, LANES), f32),
+                vmem((num_layers, 8, LANES), f32),
                 vmem((num_layers, 2 * LANES, 2 * LANES), f32),
                 vmem((2 * LANES, 2 * LANES), f32),
                 vmem((1 + 2 * num_layers, 8, LANES), f32),

time: 151 us -> 150 us (level)
  no operation moved by 1% of the time
where the time goes in v8:
time: 150 us; the launch traced here: 149 us
  Pallas kernels  144 us (96%)
  local copies, waits for them, and re-layouts  3.38 us (2%)
  between operations  1.82 us (1%)
    pallas_call x1, Pallas kernels, local_run(): pl.pallas_call(functools.partial(kernel, ny, nx, num_layers, num_qubits,...  144 us

profile of v8, /device:TPU:97, one launch (start us, length us, event | category | flops | bytes accessed | tf_op | source)
XLA Modules:
  0.0 149.5 jit_solution(14530638756541988271)
XLA Ops:
  0.6 0.0 copy-start.2
  0.6 0.0 copy-start.1
  0.6 0.6 copy-done.2
  1.3 0.0 copy-done.1
  1.3 0.0 copy-start
  1.3 0.9 copy-done
  2.3 144.3 %qaoa.1 = (f32[2,32,2,8,128]{4,3,2,1,0:T(8,128)S(1)}, f32[1,128]{1,0:T(1,128)S(1)}) custom-call(f32[32,2,8,128]{3,2,1,0:T(8,128)S(1)} %bitcast.11, f32[8]{0:T(128)S(1)} %copy-done.1, f32[8]{0:T(128)S(1)} %copy-done.2), custom_call_target="tpu_custom_call" | custom-call | tf_op jit(solution)/shard_map/qaoa/pallas_call | solution.py:588
  146.5 1.2 copy.8
  147.7 0.6 slice_bitcast_fusion
Async XLA Ops:
  0.6 0.7 copy-start.2
  0.6 0.7 copy-start.1
  1.3 0.9 copy-start

commit v9 on v8

--- a/solution.py
+++ b/solution.py
@@ -164,7 +164,7 @@
         return [(h, y * nx + x) for y in range(ny) for h in halves]
 
     def for_columns(halves, body):
-        lax.fori_loop(0, nx, lambda x, _: (body(column(x, halves)), 0)[1], 0, unroll=2)
+        lax.fori_loop(0, nx, lambda x, _: (body(column(x, halves)), 0)[1], 0, unroll=4)
 
     def load_row(ref, h, y):
         return ref[h, pl.ds(y * nx, nx), 0], ref[h, pl.ds(y * nx, nx), 1]
@@ -183,7 +183,7 @@
         return [(p[:, :LANES].reshape(nx, 8, LANES), p[:, LANES:].reshape(nx, 8, LANES)) for p in parts]
 
     def lanes_late(even, h):
-        return [] if h else waves[:1] if even else waves
+        return ([] if h else waves[:1]) if even else (waves[:1] if h else waves)
 
     def send_half(par, h, layer, tan_half, source, late):
         rows = {}

time: 150 us -> 149 us (level)
  no operation moved by 1% of the time
where the time goes in v9:
time: 149 us
  Pallas kernels  144 us (97%)
  local copies, waits for them, and re-layouts  3.38 us (2%)
  between operations  1.82 us (1%)
    pallas_call x1, Pallas kernels, local_run(): pl.pallas_call(functools.partial(kernel, ny, nx, num_layers, num_qubits,...  144 us

profile of v9, /device:TPU:97, one launch (start us, length us, event | category | flops | bytes accessed | tf_op | source)
XLA Modules:
  0.0 149.2 jit_solution(12508254139829897765)
XLA Ops:
  0.6 0.0 copy-start.2
  0.6 0.0 copy-start.1
  0.6 0.6 copy-done.2
  1.3 0.0 copy-done.1
  1.3 0.0 copy-start
  1.3 0.9 copy-done
  2.3 144.0 %qaoa.1 = (f32[2,32,2,8,128]{4,3,2,1,0:T(8,128)S(1)}, f32[1,128]{1,0:T(1,128)S(1)}) custom-call(f32[32,2,8,128]{3,2,1,0:T(8,128)S(1)} %bitcast.11, f32[8]{0:T(128)S(1)} %copy-done.1, f32[8]{0:T(128)S(1)} %copy-done.2), custom_call_target="tpu_custom_call" | custom-call | tf_op jit(solution)/shard_map/qaoa/pallas_call | solution.py:588
  146.3 1.2 copy.8
  147.5 0.6 slice_bitcast_fusion
Async XLA Ops:
  0.6 0.7 copy-start.2
  0.6 0.7 copy-start.1
  1.3 0.9 copy-start

commit v10 on v9

--- a/solution.py
+++ b/solution.py
@@ -475,16 +475,17 @@
             collect(done, cost_b)
             prepare(following)
 
-        @pl.when((k < 3) | (k == 4))
-        def _():
-            piece = k - k // 4
-            send_half(2 + piece // 2, piece % 2, 0, tan0, side, [])
-
         step = 2 * k + 1
         _, done, _, following = plan(step)
         tan_half = angle[done]
-        for h in range(2):
-            receive(1, h, done, tan_half, work, lanes_late(False, h))
+        receive(1, 0, done, tan_half, work, lanes_late(False, 0))
+
+        @pl.when((k < 3) | (k == 4))
+        def _():
+            piece = k - k // 4
+            send_half(2 + piece // 2, piece % 2, 0, tan0, side, [])
+
+        receive(1, 1, done, tan_half, work, lanes_late(False, 1))
 
         @pl.when(k % pairs < pairs - 1)
         def _():

time: 149 us -> 154 us (1.034)
  Pallas kernels: 144 us -> 148 us
    pallas_call x1, Pallas kernels: 144 us -> 148 us  [local_run(): pl.pallas_call(functools.partial(kernel, ny, nx, num_layers, num_qubits,...]
where the time goes in v10:
time: 154 us
  Pallas kernels  148 us (96%)
  local copies, waits for them, and re-layouts  3.38 us (2%)
  between operations  1.82 us (1%)
    pallas_call x1, Pallas kernels, local_run(): pl.pallas_call(functools.partial(kernel, ny, nx, num_layers, num_qubits,...  148 us

profile of v10, /device:TPU:97, one launch (start us, length us, event | category | flops | bytes accessed | tf_op | source)
XLA Modules:
  0.0 153.7 jit_solution(15238179997157381630)
XLA Ops:
  0.6 0.0 copy-start.2
  0.6 0.0 copy-start.1
  0.6 0.6 copy-done.2
  1.3 0.0 copy-done.1
  1.3 0.0 copy-start
  1.3 0.9 copy-done
  2.3 148.4 %qaoa.1 = (f32[2,32,2,8,128]{4,3,2,1,0:T(8,128)S(1)}, f32[1,128]{1,0:T(1,128)S(1)}) custom-call(f32[32,2,8,128]{3,2,1,0:T(8,128)S(1)} %bitcast.11, f32[8]{0:T(128)S(1)} %copy-done.1, f32[8]{0:T(128)S(1)} %copy-done.2), custom_call_target="tpu_custom_call" | custom-call | tf_op jit(solution)/shard_map/qaoa/pallas_call | solution.py:589
  150.7 1.2 copy.8
  151.9 0.6 slice_bitcast_fusion
Async XLA Ops:
  0.6 0.7 copy-start.2
  0.6 0.7 copy-start.1
  1.3 0.9 copy-start
